TPU v7x, 32 devices: a whole 2x2x4 slice. The times are simulated.
32 devices in a mesh: dp: 2 (over core), expert: 4 (over y, x), mp: 4 (over z).
Axes of the slice: x: 2, y: 2, z: 4, core: 2. Of those that a mesh axis runs over, the one named last changes fastest.
Arguments:
- hidden: bfloat16 [3072, 2, 7168], P(('dp', 'expert'), None, 'mp'), may hold values from -6 to 6
- cotangent: bfloat16 [3072, 2048], P(('dp', 'expert'), 'mp'), may hold values from -6 to 6
- routes: int32 [3072, 2], P(('dp', 'expert')), may hold values from 0 to 3, all different within a row; in each aligned block of 384 rows (0 to 383, 384 to 767, ...) at most 288 rows name the same one
- combine: float32 [3072, 2], P(('dp', 'expert')), may hold values from 0.1 to 0.9
- block_pair: int32 [8, 12], P(('dp', 'expert')), may hold values from 0 to 11, each once within a row
- lengths: int32 [8, 12], P(('dp', 'expert')), may hold values from 4 to 32
- log_ratio: float32 [8, 12], P(('dp', 'expert')), may hold values from -30 to 30
Outputs:
- grad_down: float32 [4, 7168, 2048], P('expert', ('mp', 'dp'))
- expert_load: float32 [4], replicated
Inputs may be any that keep to these rules, and one draw needn't show every extreme that they name: `routes`: each row names 2 different experts; in each aligned block of 384 rows (the rows of one device) no expert is named more than 288 times, and in some blocks one expert is named exactly 288 times. `block_pair`: each row holds every number of 0 to 11 once; value v marks the chosen response of the row's pair v // 2 if v is even, its rejected response if v is odd.
All inputs are finite; a program needn't handle non-finite values.
Results may differ from a plain program's by a relative error of at most 0.0029.
Values may be sent and summed in bfloat16 or wider, within the bound.
A program may use at most 128 MiB of HBM per device.

v0:
```python
import functools

import jax
import jax.numpy as jnp
from jax import lax
from jax.experimental import pallas as pl
from jax.experimental.pallas import tpu as pltpu
from jax.sharding import PartitionSpec as P

EXP_DEV = 1
LEN = 32
LANES = 128
VMEM_ROOM = 48 * 1024 * 1024
VMEM_MOST = 67043328
MESH = pl.DeviceIdType.MESH


beta_scale = 0.1


def token_factors(block_pair, lengths, log_ratio, block_len):
    blocks = block_pair.shape[1]
    labels = jnp.arange(blocks, dtype=jnp.int32)
    matches = block_pair[:, :, None] == labels[None, None, :]
    by_label = jnp.sum(jnp.where(matches, log_ratio[:, :, None], 0.0), axis=1)
    margin = by_label[:, 0::2] - by_label[:, 1::2]
    pair_coef = beta_scale * jax.nn.sigmoid(-beta_scale * margin)
    owners = block_pair // 2
    pair_ids = jnp.arange(blocks // 2, dtype=jnp.int32)
    picked = owners[:, :, None] == pair_ids[None, None, :]
    block_coef = jnp.sum(jnp.where(picked, pair_coef[:, None, :], 0.0), axis=2)
    block_weight = jnp.where(block_pair % 2 == 0, -block_coef, block_coef)
    position = jnp.arange(block_len, dtype=jnp.int32)
    within = position[None, None, :] < lengths[:, :, None]
    per_token = jnp.where(within, block_weight[:, :, None], 0.0).reshape(-1)
    return per_token, within.reshape(-1)


def exchange_kernel(
    dims, h_hbm, cot_hbm, routes_hbm, combine_hbm, pair_hbm, len_hbm, ratio_hbm,
    ht_out, acc_out, last_out, sb_out, load_ref,
    h_in, cot_ref, routes_ref, combine_ref, pair_ref, len_ref, ratio_ref,
    hr, sa, sb, ht, stage,
    hs, sas, sbs, cotb, lbuf, in_sem, out_sem,
    xa_s, a_r, up_s, dn_s, dd_s, cb_s, cb_r, xb_s, b_r, db_s, h_s, h_r, l_s, l_r,
):
    nd, ne, nm, most, ca, cb = dims
    d, e, m = lax.axis_index("dp"), lax.axis_index("expert"), lax.axis_index("mp")
    toks, top, ff = h_in.shape
    half = ff // nd
    me = d * ne + e

    def dev(dd=None, ee=None, mm=None):
        return {"dp": d if dd is None else dd, "expert": e if ee is None else ee, "mp": m if mm is None else mm}

    def remote(src, dst, ssem, rsem, where):
        return pltpu.make_async_remote_copy(
            src_ref=src, dst_ref=dst, send_sem=ssem, recv_sem=rsem, device_id=where, device_id_type=MESH
        )

    loads = [
        pltpu.make_async_copy(src, dst, in_sem.at[i])
        for i, (src, dst) in enumerate((
            (pair_hbm, pair_ref), (len_hbm, len_ref), (ratio_hbm, ratio_ref), (routes_hbm, routes_ref),
            (combine_hbm, combine_ref), (cot_hbm, cot_ref), (h_hbm, h_in),
        ))
    ]
    for load in loads:
        load.start()
    barrier = pltpu.get_barrier_semaphore()
    peers = [
        dev(dd=lax.rem(d + i, nd), ee=lax.rem(e + j, ne)) for i in range(nd) for j in range(ne) if i or j
    ] + [dev(mm=lax.rem(m + i, nm)) for i in range(1, nm)]
    for peer in peers:
        pl.semaphore_signal(barrier, inc=1, device_id=peer, device_id_type=MESH)

    def ranks(named, n):
        before = lax.broadcasted_iota(jnp.int32, (n, n), 0) < lax.broadcasted_iota(jnp.int32, (n, n), 1)
        rank = jnp.dot(
            jnp.where(named, 1.0, 0.0).astype(jnp.bfloat16),
            jnp.where(before, 1.0, 0.0).astype(jnp.bfloat16),
            preferred_element_type=jnp.float32,
        )
        return jnp.where(named, rank, -1.0)

    for load in loads[:-1]:
        load.wait()

    blocks = pair_ref.shape[1]
    block_len = toks // blocks
    square = (blocks, blocks)
    diagonal = lax.broadcasted_iota(jnp.int32, square, 0) == lax.broadcasted_iota(jnp.int32, square, 1)

    def column(row):
        return jnp.sum(jnp.where(diagonal, row, 0.0), axis=1, keepdims=True)

    pair, ratio = pair_ref[...], ratio_ref[...]
    chosen = lax.rem(pair, 2) == 0
    other_side = jnp.where(chosen, pair + 1, pair - 1)
    is_other = column(pair.astype(jnp.float32)) == other_side.astype(jnp.float32)
    other_ratio = jnp.sum(jnp.where(is_other, column(ratio), 0.0), axis=0, keepdims=True)
    margin = jnp.where(chosen, ratio - other_ratio, other_ratio - ratio)
    coef = beta_scale * (1.0 / (1.0 + jnp.exp(beta_scale * margin)))
    block_weight = column(jnp.where(chosen, -coef, coef))
    token_id = lax.broadcasted_iota(jnp.int32, (blocks, toks), 1)
    place = token_id - block_len * lax.broadcasted_iota(jnp.int32, (blocks, toks), 0)
    inside = (place >= 0) & (place < block_len)
    alive = inside & (place.astype(jnp.float32) < column(len_ref[...].astype(jnp.float32)))
    live = jnp.sum(jnp.where(alive, 1.0, 0.0), axis=0, keepdims=True)
    per_token = jnp.sum(jnp.where(alive, block_weight, 0.0), axis=0, keepdims=True)
    weight = combine_ref[...] * per_token

    rows8 = -(-ne // 8) * 8
    row_id = lax.broadcasted_iota(jnp.int32, (rows8, 1), 0)
    owner = jnp.where(row_id < ne, lax.rem(row_id + e, ne), -1)
    hit0 = routes_ref[0:1, :] == owner
    hit1 = routes_ref[1:2, :] == owner
    named = hit0 | hit1
    tok_rank = ranks(named, toks)
    tok_pos = tok_rank.astype(jnp.int32)
    tok_weight = jnp.where(hit0, weight[0:1, :], 0.0) + jnp.where(hit1, weight[1:2, :], 0.0)
    in_order = (routes_ref[0:1, :] == row_id) | (routes_ref[1:2, :] == row_id)
    counts = jnp.sum(jnp.where(in_order, live, 0.0), axis=1, keepdims=True)
    lanes8 = lax.broadcasted_iota(jnp.int32, (rows8, LANES), 1) == row_id
    lbuf[me] = jnp.broadcast_to(jnp.sum(jnp.where(lanes8, counts, 0.0), axis=0, keepdims=True), (rows8, LANES))

    slot_tok = lax.broadcasted_iota(jnp.int32, (most, toks), 0)
    picks, scales = [], []
    for j in range(ne):
        hit = slot_tok == tok_pos[j : j + 1, :]
        picks.append(jnp.where(hit, 1.0, 0.0).astype(jnp.bfloat16))
        scales.append(jnp.sum(jnp.where(hit, tok_weight[j : j + 1, :], 0.0), axis=1, keepdims=True))

    def pack_s(j, rows):
        rows = jnp.dot(picks[j], rows, preferred_element_type=jnp.float32)
        return (scales[j] * rows).astype(jnp.bfloat16)

    sends = []
    for j in range(ne):
        block = pack_s(j, cot_ref[:, :ca])
        if j == 0:
            sa[m, me] = block
        else:
            sas[j] = block
    cotb[m] = cot_ref[:, ca:]

    pl.semaphore_wait(barrier, len(peers))

    for j in range(1, ne):
        copy = remote(sas.at[j], sa.at[m, me], xa_s.at[j], a_r.at[m, me], dev(ee=lax.rem(e + j, ne)))
        copy.start()
        sends.append(copy)
    for i in range(1, nm):
        copy = remote(cot_ref.at[:, pl.ds(ca, cb)], cotb.at[m], cb_s.at[i], cb_r.at[m], dev(mm=lax.rem(m + i, nm)))
        copy.start()
        sends.append(copy)
    n = 0
    for i in range(nd):
        for j in range(ne):
            if i or j:
                copy = remote(
                    lbuf.at[me], lbuf.at[me], l_s.at[n], l_r.at[me], dev(dd=lax.rem(d + i, nd), ee=lax.rem(e + j, ne))
                )
                copy.start()
                sends.append(copy)
                n += 1

    guarded = []

    def forward(q, src, up, down, ek):
        block = sa.at[q, src]
        cu = remote(block, block, up_s.at[q, ek], a_r.at[q, src], dev(mm=lax.rem(m + 1, nm)))
        cd = remote(block, block, dn_s.at[q, ek], a_r.at[q, src], dev(mm=lax.rem(m + nm - 1, nm)))

        @pl.when(up)
        def _():
            cu.start()

        @pl.when(down)
        def _():
            cd.start()

        guarded.append((up, cu))
        guarded.append((down, cd))

    def to_partners(q, src, ek, guard=None):
        for i in range(1, nd):
            c = remote(sa.at[q, src], sa.at[q, src], dd_s.at[q, i - 1, ek], a_r.at[q, src], dev(dd=lax.rem(d + i, nd)))
            if guard is None:
                c.start()
                sends.append(c)
            else:
                pl.when(guard)(c.start)
                guarded.append((guard, c))

    forward(m, me, m + 1 < nm, m > 0, e)
    to_partners(m, me, e)

    slot_flat = lax.broadcasted_iota(jnp.int32, (most, 2 * toks), 0)
    gap = lax.broadcasted_iota(jnp.int32, (toks, 2 * toks), 1) - 2 * lax.broadcasted_iota(
        jnp.int32, (toks, 2 * toks), 0
    )
    flat_pos = -1.0
    for k, hit in enumerate((hit0, hit1)):
        spread = jnp.where(gap == k, 1.0, 0.0).astype(jnp.bfloat16)
        value = jnp.where(hit, tok_rank + 1.0, 0.0)
        high = jnp.floor(value * (1.0 / 16.0))
        for part, unit in ((high, 16.0), (value - 16.0 * high, 1.0)):
            flat_pos += unit * jnp.dot(part.astype(jnp.bfloat16), spread, preferred_element_type=jnp.float32)
    flat_pos = flat_pos.astype(jnp.int32)
    loads[-1].wait()
    flat = (2 * toks, half)
    h_rows = [h_in[:, :, c * half : (c + 1) * half].reshape(flat) for c in range(nd)]
    for j in [*range(1, ne), 0]:
        pick = jnp.where(slot_flat == flat_pos[j : j + 1, :], 1.0, 0.0).astype(jnp.bfloat16)
        for c in range(nd):
            hs[j, c] = jnp.dot(pick, h_rows[c], preferred_element_type=jnp.float32).astype(jnp.bfloat16)
        for i in range(nd):
            to = lax.rem(d + i, nd)
            if i or j:
                copy = remote(
                    hs.at[j, to], hr.at[me], h_s.at[j, i], h_r.at[me], dev(dd=to, ee=lax.rem(e + j, ne))
                )
                copy.start()
                sends.append(copy)
    hr[me] = hs[0, d]

    def wait_in(buf, sem, guard=None):
        c = pltpu.make_async_copy(buf, buf, sem)
        if guard is None:
            c.wait()
        else:
            pl.when(guard)(c.wait)

    for i in range(1, nm):
        q = lax.rem(m + i, nm)
        wait_in(cotb.at[q], cb_r.at[q])
    dense = jnp.concatenate([cotb[q] for q in range(nm)], axis=1)
    for j in range(ne):
        block = pack_s(j, dense)
        if j == 0:
            sb[me] = block
            for i in range(1, nd):
                copy = remote(sb.at[me], sb.at[me], db_s.at[i - 1, 0], b_r.at[me], dev(dd=lax.rem(d + i, nd)))
                copy.start()
                sends.append(copy)
        else:
            sbs[j] = block
            copy = remote(sbs.at[j], sb.at[me], xb_s.at[j], b_r.at[me], dev(ee=lax.rem(e + j, ne)))
            copy.start()
            sends.append(copy)

    depth = nd * ne * most
    outs = []

    def nearest(r):
        near = jnp.minimum(m, nm - 1 - m)
        both = m + (r + 1) // 2 * (1 if r % 2 == 0 else -1)
        far = jnp.where(m < nm - 1 - m, m + r - near, m - r + near)
        return jnp.where(r <= 2 * near, both, far)

    def from_partners(q):
        for i in range(1, nd):
            for j in range(ne):
                src = lax.rem(d + i, nd) * ne + j
                wait_in(sa.at[q, src], a_r.at[q, src])

    def send_out(src, dst):
        copy = pltpu.make_async_copy(src, dst, out_sem.at[len(outs)])
        copy.start()
        outs.append(copy)

    def all_hidden():
        for i in range(nd):
            for j in range(ne):
                if i or j:
                    src = lax.rem(d + i, nd) * ne + lax.rem(e + j, ne)
                    wait_in(hr.at[src], h_r.at[src])
        ht[...] = hr[...].reshape(depth, half).T
        send_out(ht, ht_out)

    def product(r):
        q = nearest(r)
        from_partners(q)
        stage[r] = jnp.dot(ht[...], sa[q].reshape(depth, ca), preferred_element_type=jnp.float32)
        send_out(stage.at[r], acc_out.at[q])

    for j in range(1, ne):
        ej = lax.rem(e + j, ne)
        src = d * ne + ej
        wait_in(sa.at[m, src], a_r.at[m, src])
        forward(m, src, m + 1 < nm, m > 0, ej)
        to_partners(m, src, ej)
    for k in range(1, nm):
        below, above = m - k, m + k
        ql, qh = lax.rem(below + nm, nm), lax.rem(above, nm)
        for j in range(ne):
            if k == nm - 1 and j % 2 == 0:
                for r in range(j // 2 * (nm - 1) // 2, nm - 1 if j else (nm - 1) // 2):
                    if r == 0:
                        all_hidden()
                    product(r)
            ej = lax.rem(e + j, ne)
            src = d * ne + ej
            wait_in(sa.at[ql, src], a_r.at[ql, src], below >= 0)
            c = remote(sa.at[ql, src], sa.at[ql, src], up_s.at[ql, ej], a_r.at[ql, src], dev(mm=lax.rem(m + 1, nm)))
            go = (below >= 0) & (m + 1 < nm)
            pl.when(go)(c.start)
            guarded.append((go, c))
            to_partners(ql, src, ej, below >= 0)
            wait_in(sa.at[qh, src], a_r.at[qh, src], above < nm)
            c = remote(sa.at[qh, src], sa.at[qh, src], dn_s.at[qh, ej], a_r.at[qh, src], dev(mm=lax.rem(m + nm - 1, nm)))
            go = (above < nm) & (m > 0)
            pl.when(go)(c.start)
            guarded.append((go, c))
            to_partners(qh, src, ej, above < nm)

    for j in range(1, ne):
        src = d * ne + lax.rem(e + j, ne)
        wait_in(sb.at[src], b_r.at[src])
        for i in range(1, nd):
            copy = remote(sb.at[src], sb.at[src], db_s.at[i - 1, j], b_r.at[src], dev(dd=lax.rem(d + i, nd)))
            copy.start()
            sends.append(copy)

    last = nearest(nm - 1)
    from_partners(last)
    send_out(sa.at[last], last_out)
    for i in range(1, nd):
        for j in range(ne):
            src = lax.rem(d + i, nd) * ne + j
            wait_in(sb.at[src], b_r.at[src])
    send_out(sb, sb_out)
    for i in range(nd):
        for j in range(ne):
            if i or j:
                src = lax.rem(d + i, nd) * ne + lax.rem(e + j, ne)
                wait_in(lbuf.at[src], l_r.at[src])
    total = lbuf[0]
    for k in range(1, nd * ne):
        total = total + lbuf[k]
    load_ref[...] = total

    for c in outs:
        c.wait()
    for c in sends:
        c.wait_send()
    for go, c in guarded:
        pl.when(go)(c.wait_send)


def product_kernel(nm, ht_ref, acc_ref, last_ref, sb_ref, load_ref, out_ref, total_ref):
    m = lax.axis_index("mp")
    last = jnp.where(m < nm - 1 - m, nm - 1, 0)
    ca, cb = acc_ref.shape[2], sb_ref.shape[1] // nm
    width = ca + cb
    total_ref[...] = load_ref[0:1, : total_ref.shape[1]]
    tail = jnp.dot(ht_ref[...], last_ref[...], preferred_element_type=jnp.float32)
    cols = jnp.dot(ht_ref[...], sb_ref[...], preferred_element_type=jnp.float32)
    for q in range(nm):
        out_ref[0, :, q * width + ca : (q + 1) * width] = cols[:, q * cb : (q + 1) * cb]
        out_ref[0, :, q * width : q * width + ca] = jnp.where(last == q, tail, acc_ref[q])


def fast_body(hidden, cotangent, routes, combine, block_pair, lengths, log_ratio):
    nd, ne, nm = lax.axis_size("dp"), lax.axis_size("expert"), lax.axis_size("mp")
    toks, top, ff = hidden.shape
    width = cotangent.shape[1]
    most = 3 * toks // 4
    cb = width // 4 // LANES * LANES
    ca = width - cb
    half = ff // nd
    srcs = nd * ne
    rows8 = -(-ne // 8) * 8
    dims = (nd, ne, nm, most, ca, cb)
    bf16, f32 = jnp.bfloat16, jnp.float32
    vmem = pl.BlockSpec(memory_space=pltpu.VMEM)
    dma = pltpu.SemaphoreType.DMA
    depth = srcs * most
    hidden_t, done, last, dense, load = pl.pallas_call(
        functools.partial(exchange_kernel, dims),
        out_shape=(
            jax.ShapeDtypeStruct((half, depth), bf16),
            jax.ShapeDtypeStruct((nm, half, ca), f32),
            jax.ShapeDtypeStruct((srcs, most, ca), bf16),
            jax.ShapeDtypeStruct((srcs, most, nm * cb), bf16),
            jax.ShapeDtypeStruct((rows8, LANES), f32),
        ),
        in_specs=[pl.BlockSpec(memory_space=pltpu.HBM)] * 7,
        out_specs=(pl.BlockSpec(memory_space=pltpu.HBM),) * 4 + (vmem,),
        scratch_shapes=[
            pltpu.VMEM((toks, top, ff), bf16),
            pltpu.VMEM(cotangent.shape, bf16),
            pltpu.VMEM((top, toks), jnp.int32),
            pltpu.VMEM((top, toks), f32),
            pltpu.VMEM(block_pair.shape, jnp.int32),
            pltpu.VMEM(lengths.shape, jnp.int32),
            pltpu.VMEM(log_ratio.shape, f32),
            pltpu.VMEM((srcs, most, half), bf16),
            pltpu.VMEM((nm, srcs, most, ca), bf16),
            pltpu.VMEM((srcs, most, nm * cb), bf16),
            pltpu.VMEM((half, depth), bf16),
            pltpu.VMEM((nm - 1, half, ca), f32),
            pltpu.VMEM((ne, nd, most, half), bf16),
            pltpu.VMEM((ne, most, ca), bf16),
            pltpu.VMEM((ne, most, nm * cb), bf16),
            pltpu.VMEM((nm, toks, cb), bf16),
            pltpu.VMEM((srcs, rows8, LANES), f32),
            dma((7,)),
            dma((nm + 2,)),
            dma((ne,)),
            dma((nm, srcs)),
            dma((nm, ne)),
            dma((nm, ne)),
            dma((nm, nd, ne)),
            dma((nm,)),
            dma((nm,)),
            dma((ne,)),
            dma((srcs,)),
            dma((nd, ne)),
            dma((ne, nd)),
            dma((srcs,)),
            dma((srcs,)),
            dma((srcs,)),
        ],
        compiler_params=pltpu.CompilerParams(
            collective_id=0, has_side_effects=True, vmem_limit_bytes=VMEM_MOST
        ),
    )(hidden, cotangent, routes.T, combine.T, block_pair, lengths, log_ratio)
    steps = next(n for n in (4, 2, 1) if half % (16 * n) == 0 or n == 1)
    rows = half // steps
    grad_down, total = pl.pallas_call(
        functools.partial(product_kernel, nm),
        out_shape=(jax.ShapeDtypeStruct((1, half, nm * width), f32), jax.ShapeDtypeStruct((1, ne), f32)),
        grid=(steps,),
        in_specs=[
            pl.BlockSpec((rows, depth), lambda i: (i, 0)),
            pl.BlockSpec((nm, rows, ca), lambda i: (0, i, 0)),
            pl.BlockSpec((depth, ca), lambda i: (0, 0)),
            pl.BlockSpec((depth, nm * cb), lambda i: (0, 0)),
            pl.BlockSpec((rows8, LANES), lambda i: (0, 0)),
        ],
        out_specs=(
            pl.BlockSpec((1, rows, nm * width), lambda i: (0, i, 0)),
            pl.BlockSpec((1, ne), lambda i: (0, 0)),
        ),
        compiler_params=pltpu.CompilerParams(vmem_limit_bytes=VMEM_MOST),
    )(hidden_t, done, last.reshape(depth, ca), dense.reshape(depth, nm * cb), load)
    return grad_down, total.reshape(ne)


def plain_body(hidden, cotangent, routes, combine, block_pair, lengths, log_ratio):
    per_token, within = token_factors(block_pair, lengths, log_ratio, LEN)
    weight = combine * per_token[:, None]
    tok_rows = routes.shape[0]
    route_top = routes.shape[1]
    ff_local = hidden.shape[2]
    groups = lax.axis_size("expert")
    experts = groups * EXP_DEV
    most_rows = 3 * tok_rows // 4
    labels = jnp.arange(experts, dtype=jnp.int32)
    routed = routes[:, :, None] == labels[None, None, :]
    local_load = jnp.sum(jnp.where(routed & within[:, None, None], 1.0, 0.0), axis=(0, 1)).astype(
        jnp.float32
    )
    flat_rows = tok_rows * route_top
    flat_hits = routed.reshape(flat_rows, experts).astype(jnp.int32)
    rank_of = jnp.sum((jnp.cumsum(flat_hits, axis=0) - 1) * flat_hits, axis=1)
    slot_of = routes.reshape(flat_rows) * most_rows + rank_of
    source = (
        jnp.zeros((experts * most_rows,), jnp.int32)
        .at[slot_of]
        .set(jnp.arange(flat_rows, dtype=jnp.int32))
    )
    filled = jnp.zeros((experts * most_rows,), jnp.float32).at[slot_of].set(1.0)
    token_of = source // route_top
    slot_weight = jnp.take(weight.reshape(flat_rows), source) * filled
    packed_h = jnp.take(hidden.reshape(flat_rows, ff_local), source, axis=0).reshape(
        groups, EXP_DEV * most_rows, ff_local
    )
    narrow_s = (
        slot_weight[:, None] * jnp.take(cotangent, token_of, axis=0).astype(jnp.float32)
    ).astype(jnp.bfloat16)
    moved_h, narrow = (
        lax.all_to_all(packed_h, "expert", split_axis=0, concat_axis=0, tiled=True),
        lax.all_to_all(
            narrow_s.reshape(groups, EXP_DEV * most_rows, cotangent.shape[1]),
            "expert",
            split_axis=0,
            concat_axis=0,
            tiled=True,
        ),
    )
    moved_s = lax.all_gather(narrow, "mp", axis=2, tiled=True)
    moved_h = moved_h.reshape(groups, EXP_DEV, most_rows, ff_local)
    moved_s = moved_s.reshape(groups, EXP_DEV, most_rows, moved_s.shape[2])
    products = [
        lax.dot_general(
            moved_h[:, 0],
            moved_s[:, 0],
            (((0, 1), (0, 1)), ((), ())),
            preferred_element_type=jnp.float32,
        )
    ]
    owned = lax.psum_scatter(jnp.stack(products, axis=1), "dp", scatter_dimension=0, tiled=True)
    grad_down = jnp.transpose(owned, (1, 0, 2))
    expert_load = lax.psum(local_load, ("dp", "expert"))
    return (grad_down, expert_load)


def solution(mesh):
    in_specs = (
        P(("dp", "expert"), None, "mp"),
        P(("dp", "expert"), "mp"),
        P(("dp", "expert"), None),
        P(("dp", "expert"), None),
        P(("dp", "expert"), None),
        P(("dp", "expert"), None),
        P(("dp", "expert"), None),
    )
    out_specs = (P("expert", ("mp", "dp"), None), P())

    def body(hidden, cotangent, *rest):
        rows = mesh.shape["dp"] * mesh.shape["expert"] * (3 * hidden.shape[0] // 4)
        bytes_in = 2 * rows * (cotangent.shape[1] * mesh.shape["mp"] + hidden.shape[2])
        run = fast_body if 2 * bytes_in < VMEM_ROOM else plain_body
        return run(hidden, cotangent, *rest)

    return jax.shard_map(body, mesh=mesh, in_specs=in_specs, out_specs=out_specs, check_vma=False)
```

profile of v0, /device:TPU:0, one launch (start us, length us, event | category | flops | bytes accessed | tf_op | source)
XLA Modules:
  0.0 90.0 jit_solution(3660655650415910480)
XLA Ops:
  0.6 78.8 %shard_map.86 = (bf16[896,2304]{1,0:T(8,128)(2,1)}, f32[4,896,384]{2,1,0:T(8,128)}, bf16[8,288,384]{2,1,0:T(8,128)(2,1)}, bf16[8,288,512]{2,1,0:T(8,128)(2,1)}, f32[8,128]{1,0:T(8,128)}) custom-call(bf16[384,2,1792]{2,1,0:T(2,128)(2,1)} %h_hbm.1, bf16[384,512]{1,0:T(8,128)(2,1)} %cot_hbm.1, s32[2,384]{1,0:T(2,128)} %bitcast.7, f32[2,384]{1,0:T(2,128)} %bitcast.8, ...), custom_call_target="tpu_custom_call" | custom-call | tf_op jit(solution)/shard_map/pallas_call | solution.py:380
  79.4 10.6 %shard_map.87 = (f32[1,896,2048]{2,1,0:T(8,128)}, f32[1,4]{1,0:T(1,128)}) custom-call(bf16[896,2304]{1,0:T(8,128)(2,1)} %get-tuple-element.9.ht_ref, f32[4,896,384]{2,1,0:T(8,128)} %get-tuple-element.10.acc_ref, bf16[2304,384]{1,0:T(8,128)(2,1)} %bitcast.6, bf16[2304,512]{1,0:T(8,128)(2,1)} %bitcast.5, f32[8,128]{1,0:T(8,128)} %get-tuple-element.13.load_ref), custom_call_target="tpu_custom_call" | custom-call | tf_op jit(solution)/shard_map/pallas_call | solution.py:432
where the time goes:
time: 91.2 us; the launch traced here: 90 us
  Pallas kernels  89.3 us (98%)
    pallas_call x1, Pallas kernels, fast_body(): pl.pallas_call(functools.partial(exchange_kernel, dims), out_shape=(jax.S...  78.8 us
    pallas_call x1, Pallas kernels, fast_body(): pl.pallas_call(functools.partial(product_kernel, nm), out_shape=(jax.Shap...  10.6 us

commit v1 on v0

v1 whole, which is shorter than its diff:
```python
import functools

import jax
import jax.numpy as jnp
from jax import lax
from jax.experimental import pallas as pl
from jax.experimental.pallas import tpu as pltpu
from jax.sharding import PartitionSpec as P

EXP_DEV = 1
LEN = 32
LANES = 128
VMEM_ROOM = 48 * 1024 * 1024
VMEM_MOST = 67043328
MESH = pl.DeviceIdType.MESH


beta_scale = 0.1


def token_factors(block_pair, lengths, log_ratio, block_len):
    blocks = block_pair.shape[1]
    labels = jnp.arange(blocks, dtype=jnp.int32)
    matches = block_pair[:, :, None] == labels[None, None, :]
    by_label = jnp.sum(jnp.where(matches, log_ratio[:, :, None], 0.0), axis=1)
    margin = by_label[:, 0::2] - by_label[:, 1::2]
    pair_coef = beta_scale * jax.nn.sigmoid(-beta_scale * margin)
    owners = block_pair // 2
    pair_ids = jnp.arange(blocks // 2, dtype=jnp.int32)
    picked = owners[:, :, None] == pair_ids[None, None, :]
    block_coef = jnp.sum(jnp.where(picked, pair_coef[:, None, :], 0.0), axis=2)
    block_weight = jnp.where(block_pair % 2 == 0, -block_coef, block_coef)
    position = jnp.arange(block_len, dtype=jnp.int32)
    within = position[None, None, :] < lengths[:, :, None]
    per_token = jnp.where(within, block_weight[:, :, None], 0.0).reshape(-1)
    return per_token, within.reshape(-1)


def exchange_kernel(
    dims, h_hbm, cot_hbm, routes_hbm, combine_hbm, pair_hbm, len_hbm, ratio_hbm,
    acc_a, acc_b, load_ref,
    h_in, cot_ref, routes_ref, combine_ref, pair_ref, len_ref, ratio_ref,
    hr, sa, sb, hs, sas, sbs, cotb, lbuf, relay_h, relay_a, relay_b, ht, ht_end, in_sem,
    xa_s, a_r, ra_s, ra_r, up_s, dn_s, dd_s, cb_s, cb_r, xb_s, b_r, rb_s, rb_r, db_s,
    h_s, h_r, hp_s, hp_r, rh_s, rh_r, l_s, l_r,
):
    nd, ne, nm, most, ca, cb = dims
    d, e, m = lax.axis_index("dp"), lax.axis_index("expert"), lax.axis_index("mp")
    toks, top, ff = h_in.shape
    half = ff // nd
    side = 1 - d
    ex, ey, eg = e + 1 - 2 * lax.rem(e, 2), lax.rem(e + 2, ne), ne - 1 - e
    first, second = ex + d * (ey - ex), ey + d * (ex - ey)
    dests = (e, first, second, eg)

    def slot(dd, ee):
        return ee * nd + dd

    me = slot(d, e)

    def dev(dd=None, ee=None, mm=None):
        return {"dp": d if dd is None else dd, "expert": e if ee is None else ee, "mp": m if mm is None else mm}

    sends, guarded = [], []

    def remote(src, dst, ssem, rsem, where):
        return pltpu.make_async_remote_copy(
            src_ref=src, dst_ref=dst, send_sem=ssem, recv_sem=rsem, device_id=where, device_id_type=MESH
        )

    def send(src, dst, ssem, rsem, where):
        copy = remote(src, dst, ssem, rsem, where)
        copy.start()
        sends.append(copy)

    def send_if(go, src, dst, ssem, rsem, where):
        copy = remote(src, dst, ssem, rsem, where)
        pl.when(go)(copy.start)
        guarded.append((go, copy))

    def wait_in(buf, sem, guard=None):
        c = pltpu.make_async_copy(buf, buf, sem)
        if guard is None:
            c.wait()
        else:
            pl.when(guard)(c.wait)

    loads = [
        pltpu.make_async_copy(src, dst, in_sem.at[i])
        for i, (src, dst) in enumerate((
            (routes_hbm, routes_ref), (cot_hbm, cot_ref), (pair_hbm, pair_ref), (len_hbm, len_ref),
            (ratio_hbm, ratio_ref), (combine_hbm, combine_ref), (h_hbm, h_in),
        ))
    ]
    for load in loads:
        load.start()
    barrier = pltpu.get_barrier_semaphore()
    peers = [
        dev(dd=lax.rem(d + i, nd), ee=lax.rem(e + j, ne)) for i in range(nd) for j in range(ne) if i or j
    ] + [dev(mm=lax.rem(m + i, nm)) for i in range(1, nm)]
    for peer in peers:
        pl.semaphore_signal(barrier, inc=1, device_id=peer, device_id_type=MESH)

    loads[0].wait()
    rows8 = -(-ne // 8) * 8
    row_id = lax.broadcasted_iota(jnp.int32, (rows8, 1), 0)
    owner = jnp.full((rows8, 1), -1, jnp.int32)
    for j, to in enumerate(dests):
        owner = jnp.where(row_id == j, to, owner)
    hit0 = routes_ref[0:1, :] == owner
    hit1 = routes_ref[1:2, :] == owner
    named = hit0 | hit1
    before = lax.broadcasted_iota(jnp.int32, (toks, toks), 0) < lax.broadcasted_iota(jnp.int32, (toks, toks), 1)
    tok_rank = jnp.dot(
        jnp.where(named, 1.0, 0.0).astype(jnp.bfloat16),
        jnp.where(before, 1.0, 0.0).astype(jnp.bfloat16),
        preferred_element_type=jnp.float32,
    )
    tok_rank = jnp.where(named, tok_rank, -1.0)
    tok_pos = tok_rank.astype(jnp.int32)

    for load in loads[2:-1]:
        load.wait()

    blocks = pair_ref.shape[1]
    block_len = toks // blocks
    square = (blocks, blocks)
    diagonal = lax.broadcasted_iota(jnp.int32, square, 0) == lax.broadcasted_iota(jnp.int32, square, 1)

    def column(row):
        return jnp.sum(jnp.where(diagonal, row, 0.0), axis=1, keepdims=True)

    pair, ratio = pair_ref[...], ratio_ref[...]
    chosen = lax.rem(pair, 2) == 0
    other_side = jnp.where(chosen, pair + 1, pair - 1)
    is_other = column(pair.astype(jnp.float32)) == other_side.astype(jnp.float32)
    other_ratio = jnp.sum(jnp.where(is_other, column(ratio), 0.0), axis=0, keepdims=True)
    margin = jnp.where(chosen, ratio - other_ratio, other_ratio - ratio)
    coef = beta_scale * (1.0 / (1.0 + jnp.exp(beta_scale * margin)))
    block_weight = column(jnp.where(chosen, -coef, coef))
    token_id = lax.broadcasted_iota(jnp.int32, (blocks, toks), 1)
    place = token_id - block_len * lax.broadcasted_iota(jnp.int32, (blocks, toks), 0)
    inside = (place >= 0) & (place < block_len)
    alive = inside & (place.astype(jnp.float32) < column(len_ref[...].astype(jnp.float32)))
    live = jnp.sum(jnp.where(alive, 1.0, 0.0), axis=0, keepdims=True)
    per_token = jnp.sum(jnp.where(alive, block_weight, 0.0), axis=0, keepdims=True)
    weight = combine_ref[...] * per_token
    tok_weight = jnp.where(hit0, weight[0:1, :], 0.0) + jnp.where(hit1, weight[1:2, :], 0.0)

    loads[1].wait()
    cotb[m] = cot_ref[:, ca:]
    slot_tok = lax.broadcasted_iota(jnp.int32, (most, toks), 0)
    picks, scales = {}, {}

    def pack_s(j, rows):
        if j not in picks:
            hit = slot_tok == tok_pos[j : j + 1, :]
            picks[j] = jnp.where(hit, 1.0, 0.0).astype(jnp.bfloat16)
            scales[j] = jnp.sum(jnp.where(hit, tok_weight[j : j + 1, :], 0.0), axis=1, keepdims=True)
        rows = jnp.dot(picks[j], rows, preferred_element_type=jnp.float32)
        return (scales[j] * rows).astype(jnp.bfloat16)

    sas[3] = pack_s(3, cot_ref[:, :ca])
    pl.semaphore_wait(barrier, len(peers))
    for i in range(1, nm):
        send(cot_ref.at[:, pl.ds(ca, cb)], cotb.at[m], cb_s.at[i], cb_r.at[m], dev(mm=lax.rem(m + i, nm)))
    send(sas.at[3], relay_a, xa_s.at[3], ra_r.at[0], dev(ee=first))
    sas[2] = pack_s(2, cot_ref[:, :ca])
    send(sas.at[2], sa.at[m, me], xa_s.at[2], a_r.at[m, me], dev(ee=second))
    sas[1] = pack_s(1, cot_ref[:, :ca])
    send(sas.at[1], sa.at[m, me], xa_s.at[1], a_r.at[m, me], dev(ee=first))
    sa[m, me] = pack_s(0, cot_ref[:, :ca])

    def to_partner(q, src, ek, guard=None):
        go = (guard is None) or guard
        args = (sa.at[q, src], sa.at[q, src], dd_s.at[q, ek], a_r.at[q, src], dev(dd=side))
        if guard is None:
            send(*args)
        else:
            send_if(go, *args)

    def spread(ej):
        src = slot(d, ej)
        block = sa.at[m, src]
        send_if(m + 1 < nm, block, block, up_s.at[m, ej], a_r.at[m, src], dev(mm=lax.rem(m + 1, nm)))
        send_if(m > 0, block, block, dn_s.at[m, ej], a_r.at[m, src], dev(mm=lax.rem(m + nm - 1, nm)))
        to_partner(m, src, ej)

    def pass_on(k, ej):
        below, above = m - k, m + k
        ql, qh = lax.rem(below + nm, nm), lax.rem(above, nm)
        src = slot(d, ej)
        low, high = sa.at[ql, src], sa.at[qh, src]
        wait_in(low, a_r.at[ql, src], below >= 0)
        go = (below >= 0) & (m + 1 < nm)
        send_if(go, low, low, up_s.at[ql, ej], a_r.at[ql, src], dev(mm=lax.rem(m + 1, nm)))
        to_partner(ql, src, ej, below >= 0)
        wait_in(high, a_r.at[qh, src], above < nm)
        go = (above < nm) & (m > 0)
        send_if(go, high, high, dn_s.at[qh, ej], a_r.at[qh, src], dev(mm=lax.rem(m + nm - 1, nm)))
        to_partner(qh, src, ej, above < nm)

    spread(e)

    slot_flat = lax.broadcasted_iota(jnp.int32, (most, 2 * toks), 0)
    gap = lax.broadcasted_iota(jnp.int32, (toks, 2 * toks), 1) - 2 * lax.broadcasted_iota(
        jnp.int32, (toks, 2 * toks), 0
    )
    flat_pos = -1.0
    for k, hit in enumerate((hit0, hit1)):
        place_k = jnp.where(gap == k, 1.0, 0.0).astype(jnp.bfloat16)
        value = jnp.where(hit, tok_rank + 1.0, 0.0)
        high = jnp.floor(value * (1.0 / 16.0))
        for part, unit in ((high, 16.0), (value - 16.0 * high, 1.0)):
            flat_pos += unit * jnp.dot(part.astype(jnp.bfloat16), place_k, preferred_element_type=jnp.float32)
    flat_pos = flat_pos.astype(jnp.int32)
    loads[-1].wait()
    flat = (2 * toks, half)
    h_rows = [h_in[:, :, c * half : (c + 1) * half].reshape(flat) for c in range(nd)]

    def pack_h(j):
        pick = jnp.where(slot_flat == flat_pos[j : j + 1, :], 1.0, 0.0).astype(jnp.bfloat16)
        for c in range(nd):
            hs[j, c] = jnp.dot(pick, h_rows[c], preferred_element_type=jnp.float32).astype(jnp.bfloat16)

    pack_h(3)
    for c in range(nd):
        send(hs.at[3, c], relay_h.at[c], h_s.at[3, c], rh_r.at[c], dev(ee=first))
    pack_h(2)
    send(hs.at[2, d], hr.at[me], h_s.at[2, 0], h_r.at[me], dev(dd=d, ee=second))
    pack_h(0)
    send(hs.at[0, side], hr.at[me], h_s.at[0, 0], h_r.at[me], dev(dd=side))
    hr[me] = hs[0, d]

    wait_in(sa.at[m, slot(d, second)], a_r.at[m, slot(d, second)])
    spread(second)
    wait_in(relay_a, ra_r.at[0])
    from_first = slot(d, first)
    send(relay_a, sa.at[m, from_first], ra_s.at[0], a_r.at[m, from_first], dev(ee=second))
    pack_h(1)
    wait_in(sa.at[m, slot(d, first)], a_r.at[m, slot(d, first)])
    spread(first)

    in_order = (routes_ref[0:1, :] == row_id) | (routes_ref[1:2, :] == row_id)
    counts = jnp.sum(jnp.where(in_order, live, 0.0), axis=1, keepdims=True)
    lanes8 = lax.broadcasted_iota(jnp.int32, (rows8, LANES), 1) == row_id
    lbuf[me] = jnp.broadcast_to(jnp.sum(jnp.where(lanes8, counts, 0.0), axis=0, keepdims=True), (rows8, LANES))

    for i in range(1, nm):
        q = lax.rem(m + i, nm)
        wait_in(cotb.at[q], cb_r.at[q])
    dense = jnp.concatenate([cotb[q] for q in range(nm)], axis=1)
    sbs[3] = pack_s(3, dense)
    send(sbs.at[3], relay_b, xb_s.at[3], rb_r.at[0], dev(ee=first))
    sbs[2] = pack_s(2, dense)
    send(sbs.at[2], sb.at[me], xb_s.at[2], b_r.at[me], dev(ee=second))
    sbs[1] = pack_s(1, dense)
    send(sbs.at[1], sb.at[me], xb_s.at[1], b_r.at[me], dev(ee=first))
    sb[me] = pack_s(0, dense)
    send(sb.at[me], sb.at[me], db_s.at[0], b_r.at[me], dev(dd=side))

    def share_b(ej, n):
        src = slot(d, ej)
        wait_in(sb.at[src], b_r.at[src])
        send(sb.at[src], sb.at[src], db_s.at[n], b_r.at[src], dev(dd=side))

    n = 0
    for i in range(nd):
        for j in range(ne):
            if i or j:
                to = dev(dd=lax.rem(d + i, nd), ee=lax.rem(e + j, ne))
                send(lbuf.at[me], lbuf.at[me], l_s.at[n], l_r.at[me], to)
                n += 1

    whole = most // 256 * 256
    part = whole // 2
    pieces = ((0, part), (part, part), (whole, most - whole))
    send(hs.at[1, d], hr.at[me], h_s.at[1, 0], h_r.at[me], dev(dd=d, ee=first))

    def send_last(j, to, axis):
        for p, (at, rows) in enumerate(pieces):
            send(
                hs.at[j, side, pl.ds(at, rows)], hr.at[me, pl.ds(at, rows)], hp_s.at[j - 1, p], hp_r.at[axis, p],
                dev(dd=side, ee=to),
            )

    send_last(1, first, d)

    def nearest(r):
        near = jnp.minimum(m, nm - 1 - m)
        both = m + (r + 1) // 2 * (1 if r % 2 == 0 else -1)
        far = jnp.where(m < nm - 1 - m, m + r - near, m - r + near)
        return jnp.where(r <= 2 * near, both, far)

    def put(ref, index, value, fresh):
        if fresh:
            ref[index] = value
        else:
            ref[index] = ref[index] + value

    def unit(r, left, cut, fresh=False):
        if r < nm:
            q = nearest(r)
            put(acc_a, q, jnp.dot(left[...], cut(sa.at[q]), preferred_element_type=jnp.float32), fresh)
        else:
            put(acc_b, ..., jnp.dot(left[...], cut(sb), preferred_element_type=jnp.float32), fresh)

    def rows_of(s0, s1, at, rows):
        def cut(ref):
            return jnp.concatenate([ref[s0, at : at + rows], ref[s1, at : at + rows]], axis=0)

        return cut

    def turn(s0, s1, at, rows):
        return jnp.concatenate([hr[s0, at : at + rows], hr[s1, at : at + rows]], axis=0).T

    def partner_a(r, ej):
        q = nearest(r)
        src = slot(side, ej)
        wait_in(sa.at[q, src], a_r.at[q, src])

    def partner_b(ej):
        src = slot(side, ej)
        wait_in(sb.at[src], b_r.at[src])

    def wait_h(src):
        wait_in(hr.at[src], h_r.at[src])

    B = nm
    own = rows_of(slot(0, e), slot(1, e), 0, whole)
    diag = rows_of(slot(0, eg), slot(1, eg), 0, whole)
    same = rows_of(slot(d, ex), slot(d, ey), 0, whole)

    pass_on(1, e)
    wait_in(sa.at[m, slot(d, eg)], a_r.at[m, slot(d, eg)])
    spread(eg)
    pass_on(1, second)
    pass_on(1, first)
    wait_h(slot(side, e))
    ht[0] = turn(slot(0, e), slot(1, e), 0, whole)
    partner_a(0, e)
    unit(0, ht.at[0], own, True)
    wait_in(relay_h.at[0], rh_r.at[0])
    send(relay_h.at[0], hr.at[from_first], rh_s.at[0], h_r.at[from_first], dev(dd=0, ee=second))
    partner_b(e)
    unit(B, ht.at[0], own, True)
    pass_on(1, eg)
    share_b(second, 1)
    partner_a(1, e)
    unit(1, ht.at[0], own, True)
    pass_on(2, e)
    wait_in(relay_h.at[1], rh_r.at[1])
    send(relay_h.at[1], hr.at[from_first], rh_s.at[1], h_r.at[from_first], dev(dd=1, ee=second))
    pass_on(2, second)
    wait_in(relay_b, rb_r.at[0])
    send(relay_b, sb.at[from_first], rb_s.at[0], b_r.at[from_first], dev(ee=second))
    send_last(2, second, side)
    pass_on(2, first)
    pass_on(2, eg)
    partner_a(2, e)
    unit(2, ht.at[0], own, True)
    share_b(first, 2)
    pass_on(3, e)
    partner_a(3, e)
    unit(3, ht.at[0], own, True)
    wait_h(slot(0, eg))
    wait_h(slot(1, eg))
    ht[1] = turn(slot(0, eg), slot(1, eg), 0, whole)
    for r in range(nm - 2):
        partner_a(r, eg)
        unit(r, ht.at[1], diag)
    pass_on(3, second)
    partner_a(nm - 2, eg)
    unit(nm - 2, ht.at[1], diag)
    share_b(eg, 3)
    wait_h(slot(d, ex))
    wait_h(slot(d, ey))
    ht[2] = turn(slot(d, ex), slot(d, ey), 0, whole)
    for r in range(nm - 1):
        unit(r, ht.at[2], same)
    unit(B, ht.at[2], same)
    pass_on(3, first)
    unit(nm - 1, ht.at[2], same)
    partner_b(eg)
    unit(B, ht.at[1], diag)
    x_far, y_far = slot(side, ex), slot(side, ey)

    def last_piece(p):
        at, rows = pieces[p]
        for axis, src in ((0, x_far), (1, y_far)):
            wait_in(hr.at[src, pl.ds(at, rows)], hp_r.at[axis, p])

    last_piece(0)
    ht_end[...] = turn(x_far, y_far, 0, part)
    for r in range(nm):
        partner_a(r, first)
        partner_a(r, second)
        unit(r, ht_end, rows_of(x_far, y_far, 0, part))
    partner_b(first)
    partner_b(second)
    unit(B, ht_end, rows_of(x_far, y_far, 0, part))
    pass_on(3, eg)
    partner_a(nm - 1, eg)
    unit(nm - 1, ht.at[1], diag)
    last_piece(1)
    ht_end[...] = turn(x_far, y_far, part, part)
    for r in range(nm + 1):
        unit(r, ht_end, rows_of(x_far, y_far, part, part))
    last_piece(2)
    rest = nd * ne * (most - whole)
    ht_end[...] = hr[:, whole:, :].reshape(rest, half).T
    for r in range(nm + 1):
        unit(r, ht_end, lambda ref: ref[:, whole:, :].reshape(rest, ref.shape[2]))

    for i in range(nd):
        for j in range(ne):
            if i or j:
                src = slot(lax.rem(d + i, nd), lax.rem(e + j, ne))
                wait_in(lbuf.at[src], l_r.at[src])
    total = lbuf[0]
    for k in range(1, nd * ne):
        total = total + lbuf[k]
    load_ref[...] = total

    for c in sends:
        c.wait_send()
    for go, c in guarded:
        pl.when(go)(c.wait_send)


def finish_kernel(nm, a_ref, b_ref, load_ref, out_ref, total_ref, sem):
    ca, cb = a_ref.shape[2], b_ref.shape[1] // nm
    width = ca + cb
    copies = []
    for q in range(nm):
        copies.append((a_ref.at[q], out_ref.at[0, :, pl.ds(q * width, ca)]))
        copies.append((b_ref.at[:, pl.ds(q * cb, cb)], out_ref.at[0, :, pl.ds(q * width + ca, cb)]))
    copies = [pltpu.make_async_copy(src, dst, sem.at[i]) for i, (src, dst) in enumerate(copies)]
    for copy in copies:
        copy.start()
    total_ref[...] = load_ref[0:1, : total_ref.shape[1]]
    for copy in copies:
        copy.wait()


def fast_body(hidden, cotangent, routes, combine, block_pair, lengths, log_ratio):
    nd, ne, nm = lax.axis_size("dp"), lax.axis_size("expert"), lax.axis_size("mp")
    toks, top, ff = hidden.shape
    width = cotangent.shape[1]
    most = 3 * toks // 4
    cb = width // 4 // LANES * LANES
    ca = width - cb
    half = ff // nd
    srcs = nd * ne
    rows8 = -(-ne // 8) * 8
    whole = most // 256 * 256
    dims = (nd, ne, nm, most, ca, cb)
    bf16, f32 = jnp.bfloat16, jnp.float32
    vmem = pl.BlockSpec(memory_space=pltpu.VMEM)
    hbm = pl.BlockSpec(memory_space=pltpu.HBM)
    dma = pltpu.SemaphoreType.DMA
    acc_a, acc_b, load = pl.pallas_call(
        functools.partial(exchange_kernel, dims),
        out_shape=(
            pltpu.VMEM((nm, half, ca), f32),
            pltpu.VMEM((half, nm * cb), f32),
            pltpu.VMEM((rows8, LANES), f32),
        ),
        in_specs=[hbm] * 7,
        out_specs=(vmem,) * 3,
        scratch_shapes=[
            pltpu.VMEM((toks, top, ff), bf16),
            pltpu.VMEM(cotangent.shape, bf16),
            pltpu.VMEM((top, toks), jnp.int32),
            pltpu.VMEM((top, toks), f32),
            pltpu.VMEM(block_pair.shape, jnp.int32),
            pltpu.VMEM(lengths.shape, jnp.int32),
            pltpu.VMEM(log_ratio.shape, f32),
            pltpu.VMEM((srcs, most, half), bf16),
            pltpu.VMEM((nm, srcs, most, ca), bf16),
            pltpu.VMEM((srcs, most, nm * cb), bf16),
            pltpu.VMEM((ne, nd, most, half), bf16),
            pltpu.VMEM((ne, most, ca), bf16),
            pltpu.VMEM((ne, most, nm * cb), bf16),
            pltpu.VMEM((nm, toks, cb), bf16),
            pltpu.VMEM((srcs, rows8, LANES), f32),
            pltpu.VMEM((nd, most, half), bf16),
            pltpu.VMEM((most, ca), bf16),
            pltpu.VMEM((most, nm * cb), bf16),
            pltpu.VMEM((3, half, 2 * whole), bf16),
            pltpu.VMEM((half, whole), bf16),
            dma((7,)),
            dma((ne,)),
            dma((nm, srcs)),
            dma((1,)),
            dma((1,)),
            dma((nm, ne)),
            dma((nm, ne)),
            dma((nm, ne)),
            dma((nm,)),
            dma((nm,)),
            dma((ne,)),
            dma((srcs,)),
            dma((1,)),
            dma((1,)),
            dma((ne,)),
            dma((ne, nd)),
            dma((srcs,)),
            dma((2, 3)),
            dma((2, 3)),
            dma((nd,)),
            dma((nd,)),
            dma((srcs,)),
            dma((srcs,)),
        ],
        compiler_params=pltpu.CompilerParams(
            collective_id=0, has_side_effects=True, vmem_limit_bytes=VMEM_MOST - 10 * 1024 * 1024
        ),
    )(hidden, cotangent, routes.T, combine.T, block_pair, lengths, log_ratio)
    grad_down, total = pl.pallas_call(
        functools.partial(finish_kernel, nm),
        out_shape=(jax.ShapeDtypeStruct((1, half, nm * width), f32), jax.ShapeDtypeStruct((1, ne), f32)),
        in_specs=[vmem] * 3,
        out_specs=(hbm, vmem),
        scratch_shapes=[dma((2 * nm,))],
        compiler_params=pltpu.CompilerParams(vmem_limit_bytes=1024 * 1024),
    )(acc_a, acc_b, load)
    return grad_down, total.reshape(ne)


def plain_body(hidden, cotangent, routes, combine, block_pair, lengths, log_ratio):
    per_token, within = token_factors(block_pair, lengths, log_ratio, LEN)
    weight = combine * per_token[:, None]
    tok_rows = routes.shape[0]
    route_top = routes.shape[1]
    ff_local = hidden.shape[2]
    groups = lax.axis_size("expert")
    experts = groups * EXP_DEV
    most_rows = 3 * tok_rows // 4
    labels = jnp.arange(experts, dtype=jnp.int32)
    routed = routes[:, :, None] == labels[None, None, :]
    local_load = jnp.sum(jnp.where(routed & within[:, None, None], 1.0, 0.0), axis=(0, 1)).astype(
        jnp.float32
    )
    flat_rows = tok_rows * route_top
    flat_hits = routed.reshape(flat_rows, experts).astype(jnp.int32)
    rank_of = jnp.sum((jnp.cumsum(flat_hits, axis=0) - 1) * flat_hits, axis=1)
    slot_of = routes.reshape(flat_rows) * most_rows + rank_of
    source = (
        jnp.zeros((experts * most_rows,), jnp.int32)
        .at[slot_of]
        .set(jnp.arange(flat_rows, dtype=jnp.int32))
    )
    filled = jnp.zeros((experts * most_rows,), jnp.float32).at[slot_of].set(1.0)
    token_of = source // route_top
    slot_weight = jnp.take(weight.reshape(flat_rows), source) * filled
    packed_h = jnp.take(hidden.reshape(flat_rows, ff_local), source, axis=0).reshape(
        groups, EXP_DEV * most_rows, ff_local
    )
    narrow_s = (
        slot_weight[:, None] * jnp.take(cotangent, token_of, axis=0).astype(jnp.float32)
    ).astype(jnp.bfloat16)
    moved_h, narrow = (
        lax.all_to_all(packed_h, "expert", split_axis=0, concat_axis=0, tiled=True),
        lax.all_to_all(
            narrow_s.reshape(groups, EXP_DEV * most_rows, cotangent.shape[1]),
            "expert",
            split_axis=0,
            concat_axis=0,
            tiled=True,
        ),
    )
    moved_s = lax.all_gather(narrow, "mp", axis=2, tiled=True)
    moved_h = moved_h.reshape(groups, EXP_DEV, most_rows, ff_local)
    moved_s = moved_s.reshape(groups, EXP_DEV, most_rows, moved_s.shape[2])
    products = [
        lax.dot_general(
            moved_h[:, 0],
            moved_s[:, 0],
            (((0, 1), (0, 1)), ((), ())),
            preferred_element_type=jnp.float32,
        )
    ]
    owned = lax.psum_scatter(jnp.stack(products, axis=1), "dp", scatter_dimension=0, tiled=True)
    grad_down = jnp.transpose(owned, (1, 0, 2))
    expert_load = lax.psum(local_load, ("dp", "expert"))
    return (grad_down, expert_load)


def solution(mesh):
    in_specs = (
        P(("dp", "expert"), None, "mp"),
        P(("dp", "expert"), "mp"),
        P(("dp", "expert"), None),
        P(("dp", "expert"), None),
        P(("dp", "expert"), None),
        P(("dp", "expert"), None),
        P(("dp", "expert"), None),
    )
    out_specs = (P("expert", ("mp", "dp"), None), P())

    def body(hidden, cotangent, *rest):
        rows = mesh.shape["dp"] * mesh.shape["expert"] * (3 * hidden.shape[0] // 4)
        bytes_in = 2 * rows * (cotangent.shape[1] * mesh.shape["mp"] + hidden.shape[2])
        most = 3 * hidden.shape[0] // 4
        whole = most // 256 * 256
        square = mesh.shape["dp"] == 2 and mesh.shape["expert"] == 4 and mesh.shape["mp"] == 4
        fits = square and whole and 8 * (most - whole) == whole
        run = fast_body if fits and 2 * bytes_in < VMEM_ROOM else plain_body
        return run(hidden, cotangent, *rest)

    return jax.shard_map(body, mesh=mesh, in_specs=in_specs, out_specs=out_specs, check_vma=False)
```

time: 91.2 us -> 82 us (0.90); the launches traced: 90 us -> 81.8 us
  Pallas kernels: 89.3 us -> 81 us
    pallas_call x2, Pallas kernels: 89.3 us -> 81 us  [the longest x1 77.4 us: fast_body(): pl.pallas_call(functools.partial(exchange_kernel, dims), out_shape=(pltpu...]
where the time goes in v1:
time: 82 us; the launch traced here: 81.8 us
  Pallas kernels  81 us (99%)
    pallas_call x1, Pallas kernels, fast_body(): pl.pallas_call(functools.partial(exchange_kernel, dims), out_shape=(pltpu...  77.4 us
    pallas_call x1, Pallas kernels, fast_body(): pl.pallas_call(functools.partial(finish_kernel, nm), out_shape=(jax.Shape...  3.56 us

profile of v1, /device:TPU:0, one launch (start us, length us, event | category | flops | bytes accessed | tf_op | source)
XLA Modules:
  0.0 81.8 jit_solution(4638702998349948535)
XLA Ops:
  0.6 77.4 %shard_map.86 = (f32[4,896,384]{2,1,0:T(8,128)S(1)}, f32[896,512]{1,0:T(8,128)S(1)}, f32[8,128]{1,0:T(8,128)S(1)}) custom-call(bf16[384,2,1792]{2,1,0:T(2,128)(2,1)} %h_hbm.1, bf16[384,512]{1,0:T(8,128)(2,1)} %cot_hbm.1, s32[2,384]{1,0:T(2,128)} %bitcast.3, f32[2,384]{1,0:T(2,128)} %bitcast.4, s32[1,12]{1,0:T(1,128)} %pair_hbm.1, s32[1,12]{1,0:T(1,128)} %len_hbm.1, ...), custom_call_target="tpu_custom_call" | custom-call | tf_op jit(solution)/shard_map/pallas_call | solution.py:462
  78.1 3.6 %shard_map.87 = (f32[1,896,2048]{2,1,0:T(8,128)}, f32[1,4]{1,0:T(1,128)}) custom-call(f32[4,896,384]{2,1,0:T(8,128)S(1)} %get-tuple-element.7.a_ref, f32[896,512]{1,0:T(8,128)S(1)} %get-tuple-element.8.b_ref, f32[8,128]{1,0:T(8,128)S(1)} %get-tuple-element.9.load_ref), custom_call_target="tpu_custom_call" | custom-call | tf_op jit(solution)/shard_map/pallas_call | solution.py:520

commit v2 on v1

--- a/solution.py
+++ b/solution.py
@@ -38,11 +38,11 @@
 
 def exchange_kernel(
     dims, h_hbm, cot_hbm, routes_hbm, combine_hbm, pair_hbm, len_hbm, ratio_hbm,
-    acc_a, acc_b, load_ref,
+    acc_a, acc_b, ht_end, end_a, end_b, load_ref,
     h_in, cot_ref, routes_ref, combine_ref, pair_ref, len_ref, ratio_ref,
-    hr, sa, sb, hs, sas, sbs, cotb, lbuf, relay_h, relay_a, relay_b, ht, ht_end, in_sem,
-    xa_s, a_r, ra_s, ra_r, up_s, dn_s, dd_s, cb_s, cb_r, xb_s, b_r, rb_s, rb_r, db_s,
-    h_s, h_r, hp_s, hp_r, rh_s, rh_r, l_s, l_r,
+    hr, sa, sb, hs, sas, sbs, cotb, lbuf, relay_h, relay_a, relay_b, raw_a, raw_b, meta_out, meta_in, ht, ht_far,
+    in_sem, xa_s, a_r, ra_s, rw_s, rw_r, up_s, dn_s, dd_s, cb_s, cb_r, xb_s, b_r, rb_s, db_s,
+    h_s, h_r, he_s, he_r, rh_s, rh_r, re_s, l_s, l_r,
 ):
     nd, ne, nm, most, ca, cb = dims
     d, e, m = lax.axis_index("dp"), lax.axis_index("expert"), lax.axis_index("mp")
@@ -149,27 +149,27 @@
 
     loads[1].wait()
     cotb[m] = cot_ref[:, ca:]
+    meta_out[...] = jnp.concatenate([tok_rank[:ne], tok_weight[:ne]], axis=0)
     slot_tok = lax.broadcasted_iota(jnp.int32, (most, toks), 0)
-    picks, scales = {}, {}
-
-    def pack_s(j, rows):
-        if j not in picks:
-            hit = slot_tok == tok_pos[j : j + 1, :]
-            picks[j] = jnp.where(hit, 1.0, 0.0).astype(jnp.bfloat16)
-            scales[j] = jnp.sum(jnp.where(hit, tok_weight[j : j + 1, :], 0.0), axis=1, keepdims=True)
-        rows = jnp.dot(picks[j], rows, preferred_element_type=jnp.float32)
-        return (scales[j] * rows).astype(jnp.bfloat16)
-
-    sas[3] = pack_s(3, cot_ref[:, :ca])
     pl.semaphore_wait(barrier, len(peers))
+    send(cot_ref.at[:, pl.ds(0, ca)], raw_a, rw_s.at[0], rw_r.at[0], dev(ee=first))
     for i in range(1, nm):
         send(cot_ref.at[:, pl.ds(ca, cb)], cotb.at[m], cb_s.at[i], cb_r.at[m], dev(mm=lax.rem(m + i, nm)))
-    send(sas.at[3], relay_a, xa_s.at[3], ra_r.at[0], dev(ee=first))
-    sas[2] = pack_s(2, cot_ref[:, :ca])
-    send(sas.at[2], sa.at[m, me], xa_s.at[2], a_r.at[m, me], dev(ee=second))
-    sas[1] = pack_s(1, cot_ref[:, :ca])
-    send(sas.at[1], sa.at[m, me], xa_s.at[1], a_r.at[m, me], dev(ee=first))
-    sa[m, me] = pack_s(0, cot_ref[:, :ca])
+    send(meta_out, meta_in, rw_s.at[1], rw_r.at[1], dev(ee=first))
+
+    def picker(position, factor):
+        hit = slot_tok == position
+        pick = jnp.where(hit, 1.0, 0.0).astype(jnp.bfloat16)
+        scale = jnp.sum(jnp.where(hit, factor, 0.0), axis=1, keepdims=True)
+
+        def pack(rows):
+            rows = jnp.dot(pick, rows, preferred_element_type=jnp.float32)
+            return (scale * rows).astype(jnp.bfloat16)
+
+        return pack
+
+    pack_own = picker(tok_pos[0:1, :], tok_weight[0:1, :])
+    sa[m, me] = pack_own(cot_ref[:, :ca])
 
     def to_partner(q, src, ek, guard=None):
         go = (guard is None) or guard
@@ -201,6 +201,9 @@
         to_partner(qh, src, ej, above < nm)
 
     spread(e)
+    pack_second = picker(tok_pos[2:3, :], tok_weight[2:3, :])
+    sas[...] = pack_second(cot_ref[:, :ca])
+    send(sas, sa.at[m, me], xa_s.at[0], a_r.at[m, me], dev(ee=second))
 
     slot_flat = lax.broadcasted_iota(jnp.int32, (most, 2 * toks), 0)
     gap = lax.broadcasted_iota(jnp.int32, (toks, 2 * toks), 1) - 2 * lax.broadcasted_iota(
@@ -223,23 +226,28 @@
         for c in range(nd):
             hs[j, c] = jnp.dot(pick, h_rows[c], preferred_element_type=jnp.float32).astype(jnp.bfloat16)
 
+    whole = most // 256 * 256
+    main, rest = pl.ds(0, whole), pl.ds(whole, most - whole)
     pack_h(3)
     for c in range(nd):
         send(hs.at[3, c], relay_h.at[c], h_s.at[3, c], rh_r.at[c], dev(ee=first))
     pack_h(2)
-    send(hs.at[2, d], hr.at[me], h_s.at[2, 0], h_r.at[me], dev(dd=d, ee=second))
+    wait_in(meta_in, rw_r.at[1])
+    wait_in(raw_a, rw_r.at[0])
+    from_first = slot(d, first)
+    pack_relay = picker(meta_in[3:4, :].astype(jnp.int32), meta_in[ne + 3 : ne + 4, :])
+    relay_a[...] = pack_relay(raw_a[...])
+    send(relay_a, sa.at[m, from_first], ra_s.at[0], a_r.at[m, from_first], dev(ee=second))
+    send(hs.at[2, d, main], hr.at[me, main], h_s.at[2, 0], h_r.at[me], dev(dd=d, ee=second))
+    pack_first = picker(meta_in[1:2, :].astype(jnp.int32), meta_in[ne + 1 : ne + 2, :])
+    sa[m, from_first] = pack_first(raw_a[...])
+    spread(first)
+    wait_in(sa.at[m, slot(d, second)], a_r.at[m, slot(d, second)])
+    spread(second)
     pack_h(0)
     send(hs.at[0, side], hr.at[me], h_s.at[0, 0], h_r.at[me], dev(dd=side))
     hr[me] = hs[0, d]
-
-    wait_in(sa.at[m, slot(d, second)], a_r.at[m, slot(d, second)])
-    spread(second)
-    wait_in(relay_a, ra_r.at[0])
-    from_first = slot(d, first)
-    send(relay_a, sa.at[m, from_first], ra_s.at[0], a_r.at[m, from_first], dev(ee=second))
     pack_h(1)
-    wait_in(sa.at[m, slot(d, first)], a_r.at[m, slot(d, first)])
-    spread(first)
 
     in_order = (routes_ref[0:1, :] == row_id) | (routes_ref[1:2, :] == row_id)
     counts = jnp.sum(jnp.where(in_order, live, 0.0), axis=1, keepdims=True)
@@ -249,14 +257,11 @@
     for i in range(1, nm):
         q = lax.rem(m + i, nm)
         wait_in(cotb.at[q], cb_r.at[q])
+    send(cotb, raw_b, rw_s.at[2], rw_r.at[2], dev(ee=first))
     dense = jnp.concatenate([cotb[q] for q in range(nm)], axis=1)
-    sbs[3] = pack_s(3, dense)
-    send(sbs.at[3], relay_b, xb_s.at[3], rb_r.at[0], dev(ee=first))
-    sbs[2] = pack_s(2, dense)
-    send(sbs.at[2], sb.at[me], xb_s.at[2], b_r.at[me], dev(ee=second))
-    sbs[1] = pack_s(1, dense)
-    send(sbs.at[1], sb.at[me], xb_s.at[1], b_r.at[me], dev(ee=first))
-    sb[me] = pack_s(0, dense)
+    sbs[...] = pack_second(dense)
+    send(sbs, sb.at[me], xb_s.at[0], b_r.at[me], dev(ee=second))
+    sb[me] = pack_own(dense)
     send(sb.at[me], sb.at[me], db_s.at[0], b_r.at[me], dev(dd=side))
 
     def share_b(ej, n):
@@ -272,19 +277,8 @@
                 send(lbuf.at[me], lbuf.at[me], l_s.at[n], l_r.at[me], to)
                 n += 1
 
-    whole = most // 256 * 256
-    part = whole // 2
-    pieces = ((0, part), (part, part), (whole, most - whole))
-    send(hs.at[1, d], hr.at[me], h_s.at[1, 0], h_r.at[me], dev(dd=d, ee=first))
-
-    def send_last(j, to, axis):
-        for p, (at, rows) in enumerate(pieces):
-            send(
-                hs.at[j, side, pl.ds(at, rows)], hr.at[me, pl.ds(at, rows)], hp_s.at[j - 1, p], hp_r.at[axis, p],
-                dev(dd=side, ee=to),
-            )
-
-    send_last(1, first, d)
+    for c, k in ((d, 0), (side, 1)):
+        send(hs.at[1, c], hr.at[me], h_s.at[1, k], h_r.at[me], dev(dd=c, ee=first))
 
     def nearest(r):
         near = jnp.minimum(m, nm - 1 - m)
@@ -326,6 +320,9 @@
     def wait_h(src):
         wait_in(hr.at[src], h_r.at[src])
 
+    def wait_main(src):
+        wait_in(hr.at[src, main], h_r.at[src])
+
     B = nm
     own = rows_of(slot(0, e), slot(1, e), 0, whole)
     diag = rows_of(slot(0, eg), slot(1, eg), 0, whole)
@@ -334,14 +331,14 @@
     pass_on(1, e)
     wait_in(sa.at[m, slot(d, eg)], a_r.at[m, slot(d, eg)])
     spread(eg)
+    pass_on(1, first)
     pass_on(1, second)
-    pass_on(1, first)
     wait_h(slot(side, e))
     ht[0] = turn(slot(0, e), slot(1, e), 0, whole)
     partner_a(0, e)
     unit(0, ht.at[0], own, True)
     wait_in(relay_h.at[0], rh_r.at[0])
-    send(relay_h.at[0], hr.at[from_first], rh_s.at[0], h_r.at[from_first], dev(dd=0, ee=second))
+    send(relay_h.at[0, main], hr.at[from_first, main], rh_s.at[0], h_r.at[from_first], dev(dd=0, ee=second))
     partner_b(e)
     unit(B, ht.at[0], own, True)
     pass_on(1, eg)
@@ -350,67 +347,68 @@
     unit(1, ht.at[0], own, True)
     pass_on(2, e)
     wait_in(relay_h.at[1], rh_r.at[1])
-    send(relay_h.at[1], hr.at[from_first], rh_s.at[1], h_r.at[from_first], dev(dd=1, ee=second))
+    send(relay_h.at[1, main], hr.at[from_first, main], rh_s.at[1], h_r.at[from_first], dev(dd=1, ee=second))
+    pass_on(2, first)
+    wait_in(raw_b, rw_r.at[2])
+    dense = jnp.concatenate([raw_b[q] for q in range(nm)], axis=1)
+    relay_b[...] = pack_relay(dense)
+    send(relay_b, sb.at[from_first], rb_s.at[0], b_r.at[from_first], dev(ee=second))
+    send(hs.at[2, side, main], hr.at[me, main], h_s.at[2, 1], h_r.at[me], dev(dd=side, ee=second))
+    for c, k in ((d, 0), (side, 1)):
+        send(hs.at[2, c, rest], hr.at[me, rest], he_s.at[k], he_r.at[me], dev(dd=c, ee=second))
+    for c in range(nd):
+        send(relay_h.at[c, rest], hr.at[from_first, rest], re_s.at[c], he_r.at[from_first], dev(dd=c, ee=second))
+    sb[from_first] = pack_first(dense)
+    send(sb.at[from_first], sb.at[from_first], db_s.at[2], b_r.at[from_first], dev(dd=side))
     pass_on(2, second)
-    wait_in(relay_b, rb_r.at[0])
-    send(relay_b, sb.at[from_first], rb_s.at[0], b_r.at[from_first], dev(ee=second))
-    send_last(2, second, side)
-    pass_on(2, first)
     pass_on(2, eg)
     partner_a(2, e)
     unit(2, ht.at[0], own, True)
-    share_b(first, 2)
     pass_on(3, e)
     partner_a(3, e)
     unit(3, ht.at[0], own, True)
-    wait_h(slot(0, eg))
-    wait_h(slot(1, eg))
+    wait_h(slot(d, first))
+    wait_main(slot(d, second))
+    ht[2] = turn(slot(d, ex), slot(d, ey), 0, whole)
+    for r in range(nm - 1):
+        unit(r, ht.at[2], same)
+    unit(B, ht.at[2], same)
+    wait_main(slot(0, eg))
+    wait_main(slot(1, eg))
     ht[1] = turn(slot(0, eg), slot(1, eg), 0, whole)
     for r in range(nm - 2):
         partner_a(r, eg)
         unit(r, ht.at[1], diag)
-    pass_on(3, second)
+    pass_on(3, first)
     partner_a(nm - 2, eg)
     unit(nm - 2, ht.at[1], diag)
     share_b(eg, 3)
-    wait_h(slot(d, ex))
-    wait_h(slot(d, ey))
-    ht[2] = turn(slot(d, ex), slot(d, ey), 0, whole)
-    for r in range(nm - 1):
-        unit(r, ht.at[2], same)
-    unit(B, ht.at[2], same)
-    pass_on(3, first)
+    pass_on(3, second)
     unit(nm - 1, ht.at[2], same)
     partner_b(eg)
     unit(B, ht.at[1], diag)
-    x_far, y_far = slot(side, ex), slot(side, ey)
-
-    def last_piece(p):
-        at, rows = pieces[p]
-        for axis, src in ((0, x_far), (1, y_far)):
-            wait_in(hr.at[src, pl.ds(at, rows)], hp_r.at[axis, p])
-
-    last_piece(0)
-    ht_end[...] = turn(x_far, y_far, 0, part)
-    for r in range(nm):
-        partner_a(r, first)
-        partner_a(r, second)
-        unit(r, ht_end, rows_of(x_far, y_far, 0, part))
-    partner_b(first)
-    partner_b(second)
-    unit(B, ht_end, rows_of(x_far, y_far, 0, part))
+
+    def far(src, wait, ej):
+        wait(src)
+        ht_far[...] = hr[src, :whole].T
+        for r in range(nm):
+            partner_a(r, ej)
+            unit(r, ht_far, lambda ref: ref[src, :whole])
+        partner_b(ej)
+        unit(B, ht_far, lambda ref: ref[src, :whole])
+
+    far(slot(side, second), wait_h, second)
     pass_on(3, eg)
+    far(slot(side, first), wait_main, first)
     partner_a(nm - 1, eg)
     unit(nm - 1, ht.at[1], diag)
-    last_piece(1)
-    ht_end[...] = turn(x_far, y_far, part, part)
-    for r in range(nm + 1):
-        unit(r, ht_end, rows_of(x_far, y_far, part, part))
-    last_piece(2)
-    rest = nd * ne * (most - whole)
-    ht_end[...] = hr[:, whole:, :].reshape(rest, half).T
-    for r in range(nm + 1):
-        unit(r, ht_end, lambda ref: ref[:, whole:, :].reshape(rest, ref.shape[2]))
+    depth = nd * ne * (most - whole)
+    for q in range(nm):
+        end_a[q] = sa[q, :, whole:, :].reshape(depth, ca)
+    end_b[...] = sb[:, whole:, :].reshape(depth, nm * cb)
+    for src in (slot(d, second), slot(side, first), slot(0, eg), slot(1, eg)):
+        wait_in(hr.at[src, rest], he_r.at[src])
+    ht_end[...] = hr[:, whole:, :].reshape(depth, half).T
 
     for i in range(nd):
         for j in range(ne):
@@ -428,16 +426,24 @@
         pl.when(go)(c.wait_send)
 
 
-def finish_kernel(nm, a_ref, b_ref, load_ref, out_ref, total_ref, sem):
+def finish_kernel(
+    nm, a_ref, b_ref, ht_ref, end_a, end_b, load_ref, out_ref, total_ref, stage_a, stage_b, sem
+):
     ca, cb = a_ref.shape[2], b_ref.shape[1] // nm
     width = ca + cb
     copies = []
+
+    def write(src, at, cols):
+        copy = pltpu.make_async_copy(src, out_ref.at[0, :, pl.ds(at, cols)], sem.at[len(copies)])
+        copy.start()
+        copies.append(copy)
+
+    stage_b[...] = b_ref[...] + jnp.dot(ht_ref[...], end_b[...], preferred_element_type=jnp.float32)
     for q in range(nm):
-        copies.append((a_ref.at[q], out_ref.at[0, :, pl.ds(q * width, ca)]))
-        copies.append((b_ref.at[:, pl.ds(q * cb, cb)], out_ref.at[0, :, pl.ds(q * width + ca, cb)]))
-    copies = [pltpu.make_async_copy(src, dst, sem.at[i]) for i, (src, dst) in enumerate(copies)]
-    for copy in copies:
-        copy.start()
+        write(stage_b.at[:, pl.ds(q * cb, cb)], q * width + ca, cb)
+    for q in range(nm):
+        stage_a[q] = a_ref[q] + jnp.dot(ht_ref[...], end_a[q], preferred_element_type=jnp.float32)
+        write(stage_a.at[q], q * width, ca)
     total_ref[...] = load_ref[0:1, : total_ref.shape[1]]
     for copy in copies:
         copy.wait()
@@ -459,15 +465,19 @@
     vmem = pl.BlockSpec(memory_space=pltpu.VMEM)
     hbm = pl.BlockSpec(memory_space=pltpu.HBM)
     dma = pltpu.SemaphoreType.DMA
-    acc_a, acc_b, load = pl.pallas_call(
+    depth = srcs * (most - whole)
+    results = pl.pallas_call(
         functools.partial(exchange_kernel, dims),
         out_shape=(
             pltpu.VMEM((nm, half, ca), f32),
             pltpu.VMEM((half, nm * cb), f32),
+            pltpu.VMEM((half, depth), bf16),
+            pltpu.VMEM((nm, depth, ca), bf16),
+            pltpu.VMEM((depth, nm * cb), bf16),
             pltpu.VMEM((rows8, LANES), f32),
         ),
         in_specs=[hbm] * 7,
-        out_specs=(vmem,) * 3,
+        out_specs=(vmem,) * 6,
         scratch_shapes=[
             pltpu.VMEM((toks, top, ff), bf16),
             pltpu.VMEM(cotangent.shape, bf16),
@@ -480,51 +490,56 @@
             pltpu.VMEM((nm, srcs, most, ca), bf16),
             pltpu.VMEM((srcs, most, nm * cb), bf16),
             pltpu.VMEM((ne, nd, most, half), bf16),
-            pltpu.VMEM((ne, most, ca), bf16),
-            pltpu.VMEM((ne, most, nm * cb), bf16),
+            pltpu.VMEM((most, ca), bf16),
+            pltpu.VMEM((most, nm * cb), bf16),
             pltpu.VMEM((nm, toks, cb), bf16),
             pltpu.VMEM((srcs, rows8, LANES), f32),
             pltpu.VMEM((nd, most, half), bf16),
             pltpu.VMEM((most, ca), bf16),
             pltpu.VMEM((most, nm * cb), bf16),
+            pltpu.VMEM((toks, ca), bf16),
+            pltpu.VMEM((nm, toks, cb), bf16),
+            pltpu.VMEM((2 * ne, toks), f32),
+            pltpu.VMEM((2 * ne, toks), f32),
             pltpu.VMEM((3, half, 2 * whole), bf16),
             pltpu.VMEM((half, whole), bf16),
             dma((7,)),
-            dma((ne,)),
+            dma((1,)),
             dma((nm, srcs)),
             dma((1,)),
-            dma((1,)),
+            dma((3,)),
+            dma((3,)),
             dma((nm, ne)),
             dma((nm, ne)),
             dma((nm, ne)),
             dma((nm,)),
             dma((nm,)),
-            dma((ne,)),
+            dma((1,)),
             dma((srcs,)),
-            dma((1,)),
             dma((1,)),
             dma((ne,)),
             dma((ne, nd)),
             dma((srcs,)),
-            dma((2, 3)),
-            dma((2, 3)),
+            dma((nd,)),
+            dma((srcs,)),
+            dma((nd,)),
             dma((nd,)),
             dma((nd,)),
             dma((srcs,)),
             dma((srcs,)),
         ],
         compiler_params=pltpu.CompilerParams(
-            collective_id=0, has_side_effects=True, vmem_limit_bytes=VMEM_MOST - 10 * 1024 * 1024
+            collective_id=0, has_side_effects=True, vmem_limit_bytes=VMEM_MOST - 12 * 1024 * 1024
         ),
     )(hidden, cotangent, routes.T, combine.T, block_pair, lengths, log_ratio)
     grad_down, total = pl.pallas_call(
         functools.partial(finish_kernel, nm),
         out_shape=(jax.ShapeDtypeStruct((1, half, nm * width), f32), jax.ShapeDtypeStruct((1, ne), f32)),
-        in_specs=[vmem] * 3,
+        in_specs=[vmem] * 6,
         out_specs=(hbm, vmem),
-        scratch_shapes=[dma((2 * nm,))],
-        compiler_params=pltpu.CompilerParams(vmem_limit_bytes=1024 * 1024),
-    )(acc_a, acc_b, load)
+        scratch_shapes=[pltpu.VMEM((nm, half, ca), f32), pltpu.VMEM((half, nm * cb), f32), dma((2 * nm,))],
+        compiler_params=pltpu.CompilerParams(vmem_limit_bytes=VMEM_MOST // 4),
+    )(*results)
     return grad_down, total.reshape(ne)
 
 

time: 82 us -> 79.3 us (0.967)
  Pallas kernels: 81 us -> 78.3 us
    pallas_call x1, Pallas kernels: 77.4 us -> 74.4 us  [fast_body(): pl.pallas_call(functools.partial(exchange_kernel, dims), out_shape=(pltpu...]
where the time goes in v2:
time: 79.3 us; the launch traced here: 79.1 us
  Pallas kernels  78.3 us (99%)
  between operations  0.8 us (1%)
    pallas_call x1, Pallas kernels, fast_body(): pl.pallas_call(functools.partial(exchange_kernel, dims), out_shape=(pltpu...  74.4 us
    pallas_call x1, Pallas kernels, fast_body(): pl.pallas_call(functools.partial(finish_kernel, nm), out_shape=(jax.Shape...  3.98 us

profile of v2, /device:TPU:0, one launch (start us, length us, event | category | flops | bytes accessed | tf_op | source)
XLA Modules:
  0.0 79.1 jit_solution(2999798955675904963)
XLA Ops:
  0.6 74.4 %shard_map.86 = (f32[4,896,384]{2,1,0:T(8,128)S(1)}, f32[896,512]{1,0:T(8,128)S(1)}, bf16[896,256]{1,0:T(8,128)(2,1)S(1)}, bf16[4,256,384]{2,1,0:T(8,128)(2,1)S(...) custom-call(bf16[384,2,1792]{2,1,0:T(2,128)(2,1)} %h_hbm.1, bf16[384,512]{1,0:T(8,128)(2,1)} %cot_hbm.1, ...), custom_call_target="tpu_custom_call" | custom-call | tf_op jit(solution)/shard_map/pallas_call | solution.py:469
  75.0 4.0 %shard_map.87 = (f32[1,896,2048]{2,1,0:T(8,128)}, f32[1,4]{1,0:T(1,128)}) custom-call(f32[4,896,384]{2,1,0:T(8,128)S(1)} %get-tuple-element.10.a_ref, f32[896,512]{1,0:T(8,128)S(1)} %get-tuple-element.11.b_ref, bf16[896,256]{1,0:T(8,128)(2,1)S(1)} %get-tuple-element.12.ht_ref, bf16[4,256,384]{2,1,0:T(8,128)(2,1)S(1)} %get-tuple-element.13.end_a, ...), custom_call_target="tpu_custom_call" | custom-call | tf_op jit(solution)/shard_map/pallas_call | solution.py:535

commit v3 on v2

--- a/solution.py
+++ b/solution.py
@@ -41,8 +41,7 @@
     acc_a, acc_b, ht_end, end_a, end_b, load_ref,
     h_in, cot_ref, routes_ref, combine_ref, pair_ref, len_ref, ratio_ref,
     hr, sa, sb, hs, sas, sbs, cotb, lbuf, relay_h, relay_a, relay_b, raw_a, raw_b, meta_out, meta_in, ht, ht_far,
-    in_sem, xa_s, a_r, ra_s, rw_s, rw_r, up_s, dn_s, dd_s, cb_s, cb_r, xb_s, b_r, rb_s, db_s,
-    h_s, h_r, he_s, he_r, rh_s, rh_r, re_s, l_s, l_r,
+    in_sem, s_s, up_s, dn_s, cu_s, cd_s, a_r, rw_r, cb_r, b_r, h_r, he_r, rh_r, l_r,
 ):
     nd, ne, nm, most, ca, cb = dims
     d, e, m = lax.axis_index("dp"), lax.axis_index("expert"), lax.axis_index("mp")
@@ -61,22 +60,20 @@
     def dev(dd=None, ee=None, mm=None):
         return {"dp": d if dd is None else dd, "expert": e if ee is None else ee, "mp": m if mm is None else mm}
 
-    sends, guarded = [], []
+    S_RAW_A, S_META, S_RAW_B, S_A, S_B, S_RELAY_A, S_RELAY_B, S_SIDE_A, S_SIDE_B, S_H, S_MAIN, S_REST, S_LOAD = range(13)
+    H_OWN, H_FIRST, H_SECOND, H_FAR_FIRST, H_FAR_SECOND, H_DIAG = range(6)
 
     def remote(src, dst, ssem, rsem, where):
         return pltpu.make_async_remote_copy(
             src_ref=src, dst_ref=dst, send_sem=ssem, recv_sem=rsem, device_id=where, device_id_type=MESH
         )
 
-    def send(src, dst, ssem, rsem, where):
-        copy = remote(src, dst, ssem, rsem, where)
-        copy.start()
-        sends.append(copy)
-
-    def send_if(go, src, dst, ssem, rsem, where):
-        copy = remote(src, dst, ssem, rsem, where)
-        pl.when(go)(copy.start)
-        guarded.append((go, copy))
+    def send(src, dst, ssem, rsem, where, go=None):
+        copy = remote(src, dst, s_s.at[ssem] if isinstance(ssem, int) else ssem, rsem, where)
+        if go is None:
+            copy.start()
+        else:
+            pl.when(go)(copy.start)
 
     def wait_in(buf, sem, guard=None):
         c = pltpu.make_async_copy(buf, buf, sem)
@@ -97,9 +94,16 @@
     barrier = pltpu.get_barrier_semaphore()
     peers = [
         dev(dd=lax.rem(d + i, nd), ee=lax.rem(e + j, ne)) for i in range(nd) for j in range(ne) if i or j
-    ] + [dev(mm=lax.rem(m + i, nm)) for i in range(1, nm)]
+    ]
     for peer in peers:
         pl.semaphore_signal(barrier, inc=1, device_id=peer, device_id_type=MESH)
+    has_up, has_down = m + 1 < nm, m > 0
+    up, down = dev(mm=lax.rem(m + 1, nm)), dev(mm=lax.rem(m + nm - 1, nm))
+    for go, peer in ((has_up, up), (has_down, down)):
+        pl.when(go)(
+            functools.partial(pl.semaphore_signal, barrier, inc=1, device_id=peer, device_id_type=MESH)
+        )
+    n_peers = len(peers) + jnp.where(has_up, 1, 0) + jnp.where(has_down, 1, 0)
 
     loads[0].wait()
     rows8 = -(-ne // 8) * 8
@@ -151,11 +155,22 @@
     cotb[m] = cot_ref[:, ca:]
     meta_out[...] = jnp.concatenate([tok_rank[:ne], tok_weight[:ne]], axis=0)
     slot_tok = lax.broadcasted_iota(jnp.int32, (most, toks), 0)
-    pl.semaphore_wait(barrier, len(peers))
-    send(cot_ref.at[:, pl.ds(0, ca)], raw_a, rw_s.at[0], rw_r.at[0], dev(ee=first))
-    for i in range(1, nm):
-        send(cot_ref.at[:, pl.ds(ca, cb)], cotb.at[m], cb_s.at[i], cb_r.at[m], dev(mm=lax.rem(m + i, nm)))
-    send(meta_out, meta_in, rw_s.at[1], rw_r.at[1], dev(ee=first))
+    pl.semaphore_wait(barrier, n_peers)
+    send(cot_ref.at[:, pl.ds(0, ca)], raw_a, S_RAW_A, rw_r.at[0], dev(ee=first))
+    own_cols = cot_ref.at[:, pl.ds(ca, cb)]
+    send(own_cols, cotb.at[m], cu_s.at[0], cb_r.at[m], up, has_up)
+    send(own_cols, cotb.at[m], cd_s.at[0], cb_r.at[m], down, has_down)
+    send(meta_out, meta_in, S_META, rw_r.at[1], dev(ee=first))
+
+    def chain(k):
+        return (m - k, lax.rem(m - k + nm, nm), m - k >= 0), (m + k, lax.rem(m + k, nm), m + k < nm)
+
+    def pass_cot(k):
+        (_, ql, low_here), (_, qh, high_here) = chain(k)
+        for q, here, sem, to, more in ((ql, low_here, cu_s, up, has_up), (qh, high_here, cd_s, down, has_down)):
+            wait_in(cotb.at[q], cb_r.at[q], here)
+            if k + 1 < nm:
+                send(cotb.at[q], cotb.at[q], sem.at[k], cb_r.at[q], to, here & more)
 
     def picker(position, factor):
         hit = slot_tok == position
@@ -171,39 +186,30 @@
     pack_own = picker(tok_pos[0:1, :], tok_weight[0:1, :])
     sa[m, me] = pack_own(cot_ref[:, :ca])
 
-    def to_partner(q, src, ek, guard=None):
-        go = (guard is None) or guard
-        args = (sa.at[q, src], sa.at[q, src], dd_s.at[q, ek], a_r.at[q, src], dev(dd=side))
-        if guard is None:
-            send(*args)
-        else:
-            send_if(go, *args)
+    def to_partner(q, src, guard=None):
+        send(sa.at[q, src], sa.at[q, src], S_SIDE_A, a_r.at[q, src], dev(dd=side), guard)
 
     def spread(ej):
         src = slot(d, ej)
         block = sa.at[m, src]
-        send_if(m + 1 < nm, block, block, up_s.at[m, ej], a_r.at[m, src], dev(mm=lax.rem(m + 1, nm)))
-        send_if(m > 0, block, block, dn_s.at[m, ej], a_r.at[m, src], dev(mm=lax.rem(m + nm - 1, nm)))
-        to_partner(m, src, ej)
+        send(block, block, up_s.at[0], a_r.at[m, src], up, has_up)
+        send(block, block, dn_s.at[0], a_r.at[m, src], down, has_down)
+        to_partner(m, src)
 
     def pass_on(k, ej):
-        below, above = m - k, m + k
-        ql, qh = lax.rem(below + nm, nm), lax.rem(above, nm)
+        (_, ql, low_here), (_, qh, high_here) = chain(k)
         src = slot(d, ej)
-        low, high = sa.at[ql, src], sa.at[qh, src]
-        wait_in(low, a_r.at[ql, src], below >= 0)
-        go = (below >= 0) & (m + 1 < nm)
-        send_if(go, low, low, up_s.at[ql, ej], a_r.at[ql, src], dev(mm=lax.rem(m + 1, nm)))
-        to_partner(ql, src, ej, below >= 0)
-        wait_in(high, a_r.at[qh, src], above < nm)
-        go = (above < nm) & (m > 0)
-        send_if(go, high, high, dn_s.at[qh, ej], a_r.at[qh, src], dev(mm=lax.rem(m + nm - 1, nm)))
-        to_partner(qh, src, ej, above < nm)
+        for q, here, sem, to, more in ((ql, low_here, up_s, up, has_up), (qh, high_here, dn_s, down, has_down)):
+            block = sa.at[q, src]
+            wait_in(block, a_r.at[q, src], here)
+            if k + 1 < nm:
+                send(block, block, sem.at[k], a_r.at[q, src], to, here & more)
+            to_partner(q, src, here)
 
     spread(e)
     pack_second = picker(tok_pos[2:3, :], tok_weight[2:3, :])
     sas[...] = pack_second(cot_ref[:, :ca])
-    send(sas, sa.at[m, me], xa_s.at[0], a_r.at[m, me], dev(ee=second))
+    send(sas, sa.at[m, me], S_A, a_r.at[m, me], dev(ee=second))
 
     slot_flat = lax.broadcasted_iota(jnp.int32, (most, 2 * toks), 0)
     gap = lax.broadcasted_iota(jnp.int32, (toks, 2 * toks), 1) - 2 * lax.broadcasted_iota(
@@ -230,22 +236,24 @@
     main, rest = pl.ds(0, whole), pl.ds(whole, most - whole)
     pack_h(3)
     for c in range(nd):
-        send(hs.at[3, c], relay_h.at[c], h_s.at[3, c], rh_r.at[c], dev(ee=first))
+        send(hs.at[3, c], relay_h.at[c], S_H, rh_r.at[c], dev(ee=first))
+    pass_cot(1)
     pack_h(2)
     wait_in(meta_in, rw_r.at[1])
     wait_in(raw_a, rw_r.at[0])
     from_first = slot(d, first)
     pack_relay = picker(meta_in[3:4, :].astype(jnp.int32), meta_in[ne + 3 : ne + 4, :])
     relay_a[...] = pack_relay(raw_a[...])
-    send(relay_a, sa.at[m, from_first], ra_s.at[0], a_r.at[m, from_first], dev(ee=second))
-    send(hs.at[2, d, main], hr.at[me, main], h_s.at[2, 0], h_r.at[me], dev(dd=d, ee=second))
+    send(relay_a, sa.at[m, from_first], S_RELAY_A, a_r.at[m, from_first], dev(ee=second))
+    send(hs.at[2, d, main], hr.at[me, main], S_MAIN, h_r.at[H_SECOND], dev(dd=d, ee=second))
     pack_first = picker(meta_in[1:2, :].astype(jnp.int32), meta_in[ne + 1 : ne + 2, :])
     sa[m, from_first] = pack_first(raw_a[...])
     spread(first)
+    pass_cot(2)
     wait_in(sa.at[m, slot(d, second)], a_r.at[m, slot(d, second)])
     spread(second)
     pack_h(0)
-    send(hs.at[0, side], hr.at[me], h_s.at[0, 0], h_r.at[me], dev(dd=side))
+    send(hs.at[0, side], hr.at[me], S_H, h_r.at[H_OWN], dev(dd=side))
     hr[me] = hs[0, d]
     pack_h(1)
 
@@ -254,31 +262,27 @@
     lanes8 = lax.broadcasted_iota(jnp.int32, (rows8, LANES), 1) == row_id
     lbuf[me] = jnp.broadcast_to(jnp.sum(jnp.where(lanes8, counts, 0.0), axis=0, keepdims=True), (rows8, LANES))
 
-    for i in range(1, nm):
-        q = lax.rem(m + i, nm)
-        wait_in(cotb.at[q], cb_r.at[q])
-    send(cotb, raw_b, rw_s.at[2], rw_r.at[2], dev(ee=first))
+    pass_cot(3)
+    send(cotb, raw_b, S_RAW_B, rw_r.at[2], dev(ee=first))
     dense = jnp.concatenate([cotb[q] for q in range(nm)], axis=1)
     sbs[...] = pack_second(dense)
-    send(sbs, sb.at[me], xb_s.at[0], b_r.at[me], dev(ee=second))
+    send(sbs, sb.at[me], S_B, b_r.at[me], dev(ee=second))
     sb[me] = pack_own(dense)
-    send(sb.at[me], sb.at[me], db_s.at[0], b_r.at[me], dev(dd=side))
-
-    def share_b(ej, n):
+    send(sb.at[me], sb.at[me], S_SIDE_B, b_r.at[me], dev(dd=side))
+
+    def share_b(ej):
         src = slot(d, ej)
         wait_in(sb.at[src], b_r.at[src])
-        send(sb.at[src], sb.at[src], db_s.at[n], b_r.at[src], dev(dd=side))
-
-    n = 0
+        send(sb.at[src], sb.at[src], S_SIDE_B, b_r.at[src], dev(dd=side))
+
     for i in range(nd):
         for j in range(ne):
             if i or j:
                 to = dev(dd=lax.rem(d + i, nd), ee=lax.rem(e + j, ne))
-                send(lbuf.at[me], lbuf.at[me], l_s.at[n], l_r.at[me], to)
-                n += 1
-
-    for c, k in ((d, 0), (side, 1)):
-        send(hs.at[1, c], hr.at[me], h_s.at[1, k], h_r.at[me], dev(dd=c, ee=first))
+                send(lbuf.at[me], lbuf.at[me], S_LOAD, l_r.at[0], to)
+
+    for c, role in ((d, H_FIRST), (side, H_FAR_FIRST)):
+        send(hs.at[1, c], hr.at[me], S_H, h_r.at[role], dev(dd=c, ee=first))
 
     def nearest(r):
         near = jnp.minimum(m, nm - 1 - m)
@@ -317,11 +321,11 @@
         src = slot(side, ej)
         wait_in(sb.at[src], b_r.at[src])
 
-    def wait_h(src):
-        wait_in(hr.at[src], h_r.at[src])
-
-    def wait_main(src):
-        wait_in(hr.at[src, main], h_r.at[src])
+    def wait_h(src, role):
+        wait_in(hr.at[src], h_r.at[role])
+
+    def wait_main(src, role):
+        wait_in(hr.at[src, main], h_r.at[role])
 
     B = nm
     own = rows_of(slot(0, e), slot(1, e), 0, whole)
@@ -333,33 +337,33 @@
     spread(eg)
     pass_on(1, first)
     pass_on(1, second)
-    wait_h(slot(side, e))
+    wait_h(slot(side, e), H_OWN)
     ht[0] = turn(slot(0, e), slot(1, e), 0, whole)
     partner_a(0, e)
     unit(0, ht.at[0], own, True)
     wait_in(relay_h.at[0], rh_r.at[0])
-    send(relay_h.at[0, main], hr.at[from_first, main], rh_s.at[0], h_r.at[from_first], dev(dd=0, ee=second))
+    send(relay_h.at[0, main], hr.at[from_first, main], S_MAIN, h_r.at[H_DIAG], dev(dd=0, ee=second))
     partner_b(e)
     unit(B, ht.at[0], own, True)
     pass_on(1, eg)
-    share_b(second, 1)
+    share_b(second)
     partner_a(1, e)
     unit(1, ht.at[0], own, True)
     pass_on(2, e)
     wait_in(relay_h.at[1], rh_r.at[1])
-    send(relay_h.at[1, main], hr.at[from_first, main], rh_s.at[1], h_r.at[from_first], dev(dd=1, ee=second))
+    send(relay_h.at[1, main], hr.at[from_first, main], S_MAIN, h_r.at[H_DIAG], dev(dd=1, ee=second))
     pass_on(2, first)
     wait_in(raw_b, rw_r.at[2])
     dense = jnp.concatenate([raw_b[q] for q in range(nm)], axis=1)
     relay_b[...] = pack_relay(dense)
-    send(relay_b, sb.at[from_first], rb_s.at[0], b_r.at[from_first], dev(ee=second))
-    send(hs.at[2, side, main], hr.at[me, main], h_s.at[2, 1], h_r.at[me], dev(dd=side, ee=second))
-    for c, k in ((d, 0), (side, 1)):
-        send(hs.at[2, c, rest], hr.at[me, rest], he_s.at[k], he_r.at[me], dev(dd=c, ee=second))
+    send(relay_b, sb.at[from_first], S_RELAY_B, b_r.at[from_first], dev(ee=second))
+    send(hs.at[2, side, main], hr.at[me, main], S_MAIN, h_r.at[H_FAR_SECOND], dev(dd=side, ee=second))
     for c in range(nd):
-        send(relay_h.at[c, rest], hr.at[from_first, rest], re_s.at[c], he_r.at[from_first], dev(dd=c, ee=second))
+        send(hs.at[2, c, rest], hr.at[me, rest], S_REST, he_r.at[0], dev(dd=c, ee=second))
+    for c in range(nd):
+        send(relay_h.at[c, rest], hr.at[from_first, rest], S_REST, he_r.at[0], dev(dd=c, ee=second))
     sb[from_first] = pack_first(dense)
-    send(sb.at[from_first], sb.at[from_first], db_s.at[2], b_r.at[from_first], dev(dd=side))
+    send(sb.at[from_first], sb.at[from_first], S_SIDE_B, b_r.at[from_first], dev(dd=side))
     pass_on(2, second)
     pass_on(2, eg)
     partner_a(2, e)
@@ -367,63 +371,74 @@
     pass_on(3, e)
     partner_a(3, e)
     unit(3, ht.at[0], own, True)
-    wait_h(slot(d, first))
-    wait_main(slot(d, second))
+    wait_h(slot(d, first), H_FIRST)
+    wait_main(slot(d, second), H_SECOND)
     ht[2] = turn(slot(d, ex), slot(d, ey), 0, whole)
     for r in range(nm - 1):
         unit(r, ht.at[2], same)
     unit(B, ht.at[2], same)
-    wait_main(slot(0, eg))
-    wait_main(slot(1, eg))
+    pairs = hr.at[pl.ds(slot(0, eg), nd), main]
+    wait_in(pairs, h_r.at[H_DIAG])
     ht[1] = turn(slot(0, eg), slot(1, eg), 0, whole)
-    for r in range(nm - 2):
+    for r in range(nm - 1):
         partner_a(r, eg)
         unit(r, ht.at[1], diag)
+    share_b(eg)
+    partner_b(eg)
+    unit(B, ht.at[1], diag)
+    ends = (slot(side, second), second), (slot(side, first), first)
+
+    def far(n, r):
+        src, ej = ends[n]
+        if r < nm:
+            partner_a(r, ej)
+        else:
+            partner_b(ej)
+        unit(r, ht_far.at[n], lambda ref: ref[src, :whole])
+
+    wait_h(ends[0][0], H_FAR_FIRST)
+    ht_far[0] = hr[ends[0][0], :whole].T
+    for r in (0, 1, 2, B):
+        far(0, r)
     pass_on(3, first)
-    partner_a(nm - 2, eg)
-    unit(nm - 2, ht.at[1], diag)
-    share_b(eg, 3)
     pass_on(3, second)
     unit(nm - 1, ht.at[2], same)
-    partner_b(eg)
-    unit(B, ht.at[1], diag)
-
-    def far(src, wait, ej):
-        wait(src)
-        ht_far[...] = hr[src, :whole].T
-        for r in range(nm):
-            partner_a(r, ej)
-            unit(r, ht_far, lambda ref: ref[src, :whole])
-        partner_b(ej)
-        unit(B, ht_far, lambda ref: ref[src, :whole])
-
-    far(slot(side, second), wait_h, second)
+    far(0, nm - 1)
+    wait_main(ends[1][0], H_FAR_SECOND)
+    ht_far[1] = hr[ends[1][0], :whole].T
+    for r in (0, 1, 2, B, 3):
+        far(1, r)
     pass_on(3, eg)
-    far(slot(side, first), wait_main, first)
     partner_a(nm - 1, eg)
     unit(nm - 1, ht.at[1], diag)
     depth = nd * ne * (most - whole)
     for q in range(nm):
         end_a[q] = sa[q, :, whole:, :].reshape(depth, ca)
     end_b[...] = sb[:, whole:, :].reshape(depth, nm * cb)
-    for src in (slot(d, second), slot(side, first), slot(0, eg), slot(1, eg)):
-        wait_in(hr.at[src, rest], he_r.at[src])
+    wait_in(hr.at[pl.ds(0, 2 * nd), rest], he_r.at[0])
     ht_end[...] = hr[:, whole:, :].reshape(depth, half).T
 
-    for i in range(nd):
-        for j in range(ne):
-            if i or j:
-                src = slot(lax.rem(d + i, nd), lax.rem(e + j, ne))
-                wait_in(lbuf.at[src], l_r.at[src])
+    others = nd * ne - 1
+    wait_in(lbuf.at[pl.ds(0, others)], l_r.at[0])
     total = lbuf[0]
     for k in range(1, nd * ne):
         total = total + lbuf[k]
     load_ref[...] = total
 
-    for c in sends:
-        c.wait_send()
-    for go, c in guarded:
-        pl.when(go)(c.wait_send)
+    for ref, sem in (
+        (cot_ref.at[:, pl.ds(0, ca)], S_RAW_A), (meta_out, S_META), (cotb, S_RAW_B), (sas, S_A), (sbs, S_B),
+        (relay_a, S_RELAY_A), (relay_b, S_RELAY_B), (sa.at[:, pl.ds(0, ne)], S_SIDE_A), (sb.at[pl.ds(0, ne)], S_SIDE_B),
+        (hr.at[pl.ds(0, 2 * nd + 1)], S_H), (hr.at[pl.ds(0, 2 * nd), main], S_MAIN),
+        (hr.at[pl.ds(0, 2 * nd), rest], S_REST), (lbuf.at[pl.ds(0, others)], S_LOAD),
+    ):
+        wait_in(ref, s_s.at[sem])
+    blocks_a = sa.at[0, pl.ds(0, ne)]
+    for k in range(nm - 1):
+        for go, sems, ref in (
+            ((m - k >= 0) & has_up, (up_s, cu_s), cotb.at[0]), ((m + k < nm) & has_down, (dn_s, cd_s), cotb.at[0])
+        ):
+            wait_in(blocks_a, sems[0].at[k], go)
+            wait_in(ref, sems[1].at[k], go)
 
 
 def finish_kernel(
@@ -502,31 +517,21 @@
             pltpu.VMEM((2 * ne, toks), f32),
             pltpu.VMEM((2 * ne, toks), f32),
             pltpu.VMEM((3, half, 2 * whole), bf16),
-            pltpu.VMEM((half, whole), bf16),
+            pltpu.VMEM((2, half, whole), bf16),
             dma((7,)),
+            dma((13,)),
+            dma((nm - 1,)),
+            dma((nm - 1,)),
+            dma((nm - 1,)),
+            dma((nm - 1,)),
+            dma((nm, srcs)),
+            dma((3,)),
+            dma((nm,)),
+            dma((srcs,)),
+            dma((6,)),
             dma((1,)),
-            dma((nm, srcs)),
+            dma((nd,)),
             dma((1,)),
-            dma((3,)),
-            dma((3,)),
-            dma((nm, ne)),
-            dma((nm, ne)),
-            dma((nm, ne)),
-            dma((nm,)),
-            dma((nm,)),
-            dma((1,)),
-            dma((srcs,)),
-            dma((1,)),
-            dma((ne,)),
-            dma((ne, nd)),
-            dma((srcs,)),
-            dma((nd,)),
-            dma((srcs,)),
-            dma((nd,)),
-            dma((nd,)),
-            dma((nd,)),
-            dma((srcs,)),
-            dma((srcs,)),
         ],
         compiler_params=pltpu.CompilerParams(
             collective_id=0, has_side_effects=True, vmem_limit_bytes=VMEM_MOST - 12 * 1024 * 1024

time: 79.3 us -> 77.8 us (0.981)
  Pallas kernels: 78.3 us -> 76.8 us
    pallas_call x1, Pallas kernels: 74.4 us -> 72.8 us  [fast_body(): pl.pallas_call(functools.partial(exchange_kernel, dims), out_shape=(pltpu...]
where the time goes in v3:
time: 77.8 us; the launch traced here: 77.6 us
  Pallas kernels  76.8 us (99%)
  between operations  0.8 us (1%)
    pallas_call x1, Pallas kernels, fast_body(): pl.pallas_call(functools.partial(exchange_kernel, dims), out_shape=(pltpu...  72.8 us
    pallas_call x1, Pallas kernels, fast_body(): pl.pallas_call(functools.partial(finish_kernel, nm), out_shape=(jax.Shape...  3.98 us

profile of v3, /device:TPU:0, one launch (start us, length us, event | category | flops | bytes accessed | tf_op | source)
XLA Modules:
  0.0 77.6 jit_solution(10326378726183331429)
XLA Ops:
  0.6 72.8 %shard_map.86 = (f32[4,896,384]{2,1,0:T(8,128)S(1)}, f32[896,512]{1,0:T(8,128)S(1)}, bf16[896,256]{1,0:T(8,128)(2,1)S(1)}, bf16[4,256,384]{2,1,0:T(8,128)(2,1)S(...) custom-call(bf16[384,2,1792]{2,1,0:T(2,128)(2,1)} %h_hbm.1, bf16[384,512]{1,0:T(8,128)(2,1)} %cot_hbm.1, ...), custom_call_target="tpu_custom_call" | custom-call | tf_op jit(solution)/shard_map/pallas_call | solution.py:484
  73.5 4.0 %shard_map.87 = (f32[1,896,2048]{2,1,0:T(8,128)}, f32[1,4]{1,0:T(1,128)}) custom-call(f32[4,896,384]{2,1,0:T(8,128)S(1)} %get-tuple-element.10.a_ref, f32[896,512]{1,0:T(8,128)S(1)} %get-tuple-element.11.b_ref, bf16[896,256]{1,0:T(8,128)(2,1)S(1)} %get-tuple-element.12.ht_ref, bf16[4,256,384]{2,1,0:T(8,128)(2,1)S(1)} %get-tuple-element.13.end_a, ...), custom_call_target="tpu_custom_call" | custom-call | tf_op jit(solution)/shard_map/pallas_call | solution.py:540

commit v4 on v3

--- a/solution.py
+++ b/solution.py
@@ -390,10 +390,10 @@
 
     def far(n, r):
         src, ej = ends[n]
-        if r < nm:
+        if n == 0 and r == B:
+            partner_b(ej)
+        elif n == 0 or r == nm - 1:
             partner_a(r, ej)
-        else:
-            partner_b(ej)
         unit(r, ht_far.at[n], lambda ref: ref[src, :whole])
 
     wait_h(ends[0][0], H_FAR_FIRST)
@@ -404,17 +404,32 @@
     pass_on(3, second)
     unit(nm - 1, ht.at[2], same)
     far(0, nm - 1)
+    depth = nd * ne * (most - whole)
+
+    def keep_end(r):
+        q = nearest(r)
+        end_a[q] = sa[q, :, whole:, :].reshape(depth, ca)
+
+    for r in range(nm - 1):
+        partner_a(r, first)
+        keep_end(r)
+    partner_b(first)
+    end_b[...] = sb[:, whole:, :].reshape(depth, nm * cb)
+
+    def last_unit():
+        partner_a(nm - 1, eg)
+        unit(nm - 1, ht.at[1], diag)
+
+    middle = has_up & has_down
+    pl.when(middle)(last_unit)
     wait_main(ends[1][0], H_FAR_SECOND)
     ht_far[1] = hr[ends[1][0], :whole].T
-    for r in (0, 1, 2, B, 3):
+    far(1, 0)
+    pass_on(3, eg)
+    for r in (1, 2, B, 3):
         far(1, r)
-    pass_on(3, eg)
-    partner_a(nm - 1, eg)
-    unit(nm - 1, ht.at[1], diag)
-    depth = nd * ne * (most - whole)
-    for q in range(nm):
-        end_a[q] = sa[q, :, whole:, :].reshape(depth, ca)
-    end_b[...] = sb[:, whole:, :].reshape(depth, nm * cb)
+    pl.when(jnp.logical_not(middle))(last_unit)
+    keep_end(nm - 1)
     wait_in(hr.at[pl.ds(0, 2 * nd), rest], he_r.at[0])
     ht_end[...] = hr[:, whole:, :].reshape(depth, half).T
 
@@ -448,17 +463,25 @@
     width = ca + cb
     copies = []
 
-    def write(src, at, cols):
-        copy = pltpu.make_async_copy(src, out_ref.at[0, :, pl.ds(at, cols)], sem.at[len(copies)])
+    def write(src, rows, at, cols):
+        copy = pltpu.make_async_copy(src, out_ref.at[0, rows, pl.ds(at, cols)], sem.at[len(copies)])
         copy.start()
         copies.append(copy)
 
+    def rows_a(q, parts):
+        rows = a_ref.shape[1] // parts
+        for p in range(parts):
+            cut = pl.ds(p * rows, rows)
+            stage_a[q, cut] = a_ref[q, cut] + jnp.dot(ht_ref[cut, :], end_a[q], preferred_element_type=jnp.float32)
+            write(stage_a.at[q, cut], cut, q * width, ca)
+
+    half = pl.ds(0, b_ref.shape[0])
+    rows_a(0, 2)
     stage_b[...] = b_ref[...] + jnp.dot(ht_ref[...], end_b[...], preferred_element_type=jnp.float32)
     for q in range(nm):
-        write(stage_b.at[:, pl.ds(q * cb, cb)], q * width + ca, cb)
-    for q in range(nm):
-        stage_a[q] = a_ref[q] + jnp.dot(ht_ref[...], end_a[q], preferred_element_type=jnp.float32)
-        write(stage_a.at[q], q * width, ca)
+        write(stage_b.at[:, pl.ds(q * cb, cb)], half, q * width + ca, cb)
+    for q in range(1, nm):
+        rows_a(q, 2 if q == nm - 1 else 1)
     total_ref[...] = load_ref[0:1, : total_ref.shape[1]]
     for copy in copies:
         copy.wait()
@@ -542,7 +565,7 @@
         out_shape=(jax.ShapeDtypeStruct((1, half, nm * width), f32), jax.ShapeDtypeStruct((1, ne), f32)),
         in_specs=[vmem] * 6,
         out_specs=(hbm, vmem),
-        scratch_shapes=[pltpu.VMEM((nm, half, ca), f32), pltpu.VMEM((half, nm * cb), f32), dma((2 * nm,))],
+        scratch_shapes=[pltpu.VMEM((nm, half, ca), f32), pltpu.VMEM((half, nm * cb), f32), dma((2 * nm + 2,))],
         compiler_params=pltpu.CompilerParams(vmem_limit_bytes=VMEM_MOST // 4),
     )(*results)
     return grad_down, total.reshape(ne)

time: 77.8 us -> 77.6 us (level)
  no operation moved by 1% of the time
where the time goes in v4:
time: 77.6 us; the launch traced here: 77.4 us
  Pallas kernels  76.6 us (99%)
  between operations  0.8 us (1%)
    pallas_call x1, Pallas kernels, fast_body(): pl.pallas_call(functools.partial(exchange_kernel, dims), out_shape=(pltpu...  72.7 us
    pallas_call x1, Pallas kernels, fast_body(): pl.pallas_call(functools.partial(finish_kernel, nm), out_shape=(jax.Shape...  3.86 us

profile of v4, /device:TPU:0, one launch (start us, length us, event | category | flops | bytes accessed | tf_op | source)
XLA Modules:
  0.0 77.4 jit_solution(13785613791879242977)
XLA Ops:
  0.6 72.7 %shard_map.86 = (f32[4,896,384]{2,1,0:T(8,128)S(1)}, f32[896,512]{1,0:T(8,128)S(1)}, bf16[896,256]{1,0:T(8,128)(2,1)S(1)}, bf16[4,256,384]{2,1,0:T(8,128)(2,1)S(...) custom-call(bf16[384,2,1792]{2,1,0:T(2,128)(2,1)} %h_hbm.1, bf16[384,512]{1,0:T(8,128)(2,1)} %cot_hbm.1, ...), custom_call_target="tpu_custom_call" | custom-call | tf_op jit(solution)/shard_map/pallas_call | solution.py:507
  73.4 3.9 %shard_map.87 = (f32[1,896,2048]{2,1,0:T(8,128)}, f32[1,4]{1,0:T(1,128)}) custom-call(f32[4,896,384]{2,1,0:T(8,128)S(1)} %get-tuple-element.10.a_ref, f32[896,512]{1,0:T(8,128)S(1)} %get-tuple-element.11.b_ref, bf16[896,256]{1,0:T(8,128)(2,1)S(1)} %get-tuple-element.12.ht_ref, bf16[4,256,384]{2,1,0:T(8,128)(2,1)S(1)} %get-tuple-element.13.end_a, ...), custom_call_target="tpu_custom_call" | custom-call | tf_op jit(solution)/shard_map/pallas_call | solution.py:563

commit v5 on v4

--- a/solution.py
+++ b/solution.py
@@ -40,7 +40,7 @@
     dims, h_hbm, cot_hbm, routes_hbm, combine_hbm, pair_hbm, len_hbm, ratio_hbm,
     acc_a, acc_b, ht_end, end_a, end_b, load_ref,
     h_in, cot_ref, routes_ref, combine_ref, pair_ref, len_ref, ratio_ref,
-    hr, sa, sb, hs, sas, sbs, cotb, lbuf, relay_h, relay_a, relay_b, raw_a, raw_b, meta_out, meta_in, ht, ht_far,
+    hr, sa, sb, hs, sas, sbs, cotb, load_out, load_in, relay_h, relay_a, relay_b, raw_a, raw_b, meta_out, meta_in, ht, ht_far,
     in_sem, s_s, up_s, dn_s, cu_s, cd_s, a_r, rw_r, cb_r, b_r, h_r, he_r, rh_r, l_r,
 ):
     nd, ne, nm, most, ca, cb = dims
@@ -60,7 +60,7 @@
     def dev(dd=None, ee=None, mm=None):
         return {"dp": d if dd is None else dd, "expert": e if ee is None else ee, "mp": m if mm is None else mm}
 
-    S_RAW_A, S_META, S_RAW_B, S_A, S_B, S_RELAY_A, S_RELAY_B, S_SIDE_A, S_SIDE_B, S_H, S_MAIN, S_REST, S_LOAD = range(13)
+    S_RAW_A, S_META, S_RAW_B, S_A, S_B, S_H, S_Q, S_LOAD = range(8)
     H_OWN, H_FIRST, H_SECOND, H_FAR_FIRST, H_FAR_SECOND, H_DIAG = range(6)
 
     def remote(src, dst, ssem, rsem, where):
@@ -92,9 +92,7 @@
     for load in loads:
         load.start()
     barrier = pltpu.get_barrier_semaphore()
-    peers = [
-        dev(dd=lax.rem(d + i, nd), ee=lax.rem(e + j, ne)) for i in range(nd) for j in range(ne) if i or j
-    ]
+    peers = [dev(dd=side)] + [dev(dd=i, ee=to) for i in range(nd) for to in (first, second)]
     for peer in peers:
         pl.semaphore_signal(barrier, inc=1, device_id=peer, device_id_type=MESH)
     has_up, has_down = m + 1 < nm, m > 0
@@ -170,7 +168,7 @@
         for q, here, sem, to, more in ((ql, low_here, cu_s, up, has_up), (qh, high_here, cd_s, down, has_down)):
             wait_in(cotb.at[q], cb_r.at[q], here)
             if k + 1 < nm:
-                send(cotb.at[q], cotb.at[q], sem.at[k], cb_r.at[q], to, here & more)
+                send(cotb.at[q], cotb.at[q], sem.at[0], cb_r.at[q], to, here & more)
 
     def picker(position, factor):
         hit = slot_tok == position
@@ -187,7 +185,7 @@
     sa[m, me] = pack_own(cot_ref[:, :ca])
 
     def to_partner(q, src, guard=None):
-        send(sa.at[q, src], sa.at[q, src], S_SIDE_A, a_r.at[q, src], dev(dd=side), guard)
+        send(sa.at[q, src], sa.at[q, src], S_A, a_r.at[q, src], dev(dd=side), guard)
 
     def spread(ej):
         src = slot(d, ej)
@@ -203,7 +201,7 @@
             block = sa.at[q, src]
             wait_in(block, a_r.at[q, src], here)
             if k + 1 < nm:
-                send(block, block, sem.at[k], a_r.at[q, src], to, here & more)
+                send(block, block, sem.at[0], a_r.at[q, src], to, here & more)
             to_partner(q, src, here)
 
     spread(e)
@@ -239,19 +237,18 @@
         send(hs.at[3, c], relay_h.at[c], S_H, rh_r.at[c], dev(ee=first))
     pass_cot(1)
     pack_h(2)
+    wait_in(sa.at[m, slot(d, second)], a_r.at[m, slot(d, second)])
+    spread(second)
     wait_in(meta_in, rw_r.at[1])
     wait_in(raw_a, rw_r.at[0])
     from_first = slot(d, first)
     pack_relay = picker(meta_in[3:4, :].astype(jnp.int32), meta_in[ne + 3 : ne + 4, :])
     relay_a[...] = pack_relay(raw_a[...])
-    send(relay_a, sa.at[m, from_first], S_RELAY_A, a_r.at[m, from_first], dev(ee=second))
-    send(hs.at[2, d, main], hr.at[me, main], S_MAIN, h_r.at[H_SECOND], dev(dd=d, ee=second))
+    send(relay_a, sa.at[m, from_first], S_A, a_r.at[m, from_first], dev(ee=second))
+    send(hs.at[2, d, main], hr.at[me, main], S_Q, h_r.at[H_SECOND], dev(dd=d, ee=second))
     pack_first = picker(meta_in[1:2, :].astype(jnp.int32), meta_in[ne + 1 : ne + 2, :])
     sa[m, from_first] = pack_first(raw_a[...])
     spread(first)
-    pass_cot(2)
-    wait_in(sa.at[m, slot(d, second)], a_r.at[m, slot(d, second)])
-    spread(second)
     pack_h(0)
     send(hs.at[0, side], hr.at[me], S_H, h_r.at[H_OWN], dev(dd=side))
     hr[me] = hs[0, d]
@@ -260,26 +257,32 @@
     in_order = (routes_ref[0:1, :] == row_id) | (routes_ref[1:2, :] == row_id)
     counts = jnp.sum(jnp.where(in_order, live, 0.0), axis=1, keepdims=True)
     lanes8 = lax.broadcasted_iota(jnp.int32, (rows8, LANES), 1) == row_id
-    lbuf[me] = jnp.broadcast_to(jnp.sum(jnp.where(lanes8, counts, 0.0), axis=0, keepdims=True), (rows8, LANES))
-
+    load_out[0] = jnp.broadcast_to(jnp.sum(jnp.where(lanes8, counts, 0.0), axis=0, keepdims=True), (rows8, LANES))
+    partners = (dev(dd=side), dev(ee=first), dev(ee=second))
+
+    def add_load(n):
+        wait_in(load_in.at[n], l_r.at[n])
+        total = load_out[n] + load_in[n]
+        if n + 1 < len(partners):
+            load_out[n + 1] = total
+            send(load_out.at[n + 1], load_in.at[n + 1], S_LOAD + n + 1, l_r.at[n + 1], partners[n + 1])
+        else:
+            load_ref[...] = total
+
+    send(load_out.at[0], load_in.at[0], S_LOAD, l_r.at[0], partners[0])
+    pass_cot(2)
     pass_cot(3)
     send(cotb, raw_b, S_RAW_B, rw_r.at[2], dev(ee=first))
     dense = jnp.concatenate([cotb[q] for q in range(nm)], axis=1)
     sbs[...] = pack_second(dense)
     send(sbs, sb.at[me], S_B, b_r.at[me], dev(ee=second))
     sb[me] = pack_own(dense)
-    send(sb.at[me], sb.at[me], S_SIDE_B, b_r.at[me], dev(dd=side))
+    send(sb.at[me], sb.at[me], S_B, b_r.at[me], dev(dd=side))
 
     def share_b(ej):
         src = slot(d, ej)
         wait_in(sb.at[src], b_r.at[src])
-        send(sb.at[src], sb.at[src], S_SIDE_B, b_r.at[src], dev(dd=side))
-
-    for i in range(nd):
-        for j in range(ne):
-            if i or j:
-                to = dev(dd=lax.rem(d + i, nd), ee=lax.rem(e + j, ne))
-                send(lbuf.at[me], lbuf.at[me], S_LOAD, l_r.at[0], to)
+        send(sb.at[src], sb.at[src], S_B, b_r.at[src], dev(dd=side))
 
     for c, role in ((d, H_FIRST), (side, H_FAR_FIRST)):
         send(hs.at[1, c], hr.at[me], S_H, h_r.at[role], dev(dd=c, ee=first))
@@ -342,35 +345,38 @@
     partner_a(0, e)
     unit(0, ht.at[0], own, True)
     wait_in(relay_h.at[0], rh_r.at[0])
-    send(relay_h.at[0, main], hr.at[from_first, main], S_MAIN, h_r.at[H_DIAG], dev(dd=0, ee=second))
+    send(relay_h.at[0, main], hr.at[from_first, main], S_Q, h_r.at[H_DIAG], dev(dd=0, ee=second))
     partner_b(e)
     unit(B, ht.at[0], own, True)
     pass_on(1, eg)
     share_b(second)
     partner_a(1, e)
     unit(1, ht.at[0], own, True)
+    add_load(0)
     pass_on(2, e)
     wait_in(relay_h.at[1], rh_r.at[1])
-    send(relay_h.at[1, main], hr.at[from_first, main], S_MAIN, h_r.at[H_DIAG], dev(dd=1, ee=second))
+    send(relay_h.at[1, main], hr.at[from_first, main], S_Q, h_r.at[H_DIAG], dev(dd=1, ee=second))
     pass_on(2, first)
     wait_in(raw_b, rw_r.at[2])
     dense = jnp.concatenate([raw_b[q] for q in range(nm)], axis=1)
     relay_b[...] = pack_relay(dense)
-    send(relay_b, sb.at[from_first], S_RELAY_B, b_r.at[from_first], dev(ee=second))
-    send(hs.at[2, side, main], hr.at[me, main], S_MAIN, h_r.at[H_FAR_SECOND], dev(dd=side, ee=second))
+    send(relay_b, sb.at[from_first], S_B, b_r.at[from_first], dev(ee=second))
+    send(hs.at[2, side, main], hr.at[me, main], S_Q, h_r.at[H_FAR_SECOND], dev(dd=side, ee=second))
     for c in range(nd):
-        send(hs.at[2, c, rest], hr.at[me, rest], S_REST, he_r.at[0], dev(dd=c, ee=second))
+        send(hs.at[2, c, rest], hr.at[me, rest], S_Q, he_r.at[0], dev(dd=c, ee=second))
     for c in range(nd):
-        send(relay_h.at[c, rest], hr.at[from_first, rest], S_REST, he_r.at[0], dev(dd=c, ee=second))
+        send(relay_h.at[c, rest], hr.at[from_first, rest], S_Q, he_r.at[0], dev(dd=c, ee=second))
     sb[from_first] = pack_first(dense)
-    send(sb.at[from_first], sb.at[from_first], S_SIDE_B, b_r.at[from_first], dev(dd=side))
+    send(sb.at[from_first], sb.at[from_first], S_B, b_r.at[from_first], dev(dd=side))
     pass_on(2, second)
     pass_on(2, eg)
     partner_a(2, e)
     unit(2, ht.at[0], own, True)
+    add_load(1)
     pass_on(3, e)
     partner_a(3, e)
     unit(3, ht.at[0], own, True)
+    add_load(2)
     wait_h(slot(d, first), H_FIRST)
     wait_main(slot(d, second), H_SECOND)
     ht[2] = turn(slot(d, ex), slot(d, ey), 0, whole)
@@ -425,35 +431,27 @@
     wait_main(ends[1][0], H_FAR_SECOND)
     ht_far[1] = hr[ends[1][0], :whole].T
     far(1, 0)
+    far(1, 1)
     pass_on(3, eg)
-    for r in (1, 2, B, 3):
+    for r in (2, B, 3):
         far(1, r)
     pl.when(jnp.logical_not(middle))(last_unit)
     keep_end(nm - 1)
     wait_in(hr.at[pl.ds(0, 2 * nd), rest], he_r.at[0])
     ht_end[...] = hr[:, whole:, :].reshape(depth, half).T
 
-    others = nd * ne - 1
-    wait_in(lbuf.at[pl.ds(0, others)], l_r.at[0])
-    total = lbuf[0]
-    for k in range(1, nd * ne):
-        total = total + lbuf[k]
-    load_ref[...] = total
-
     for ref, sem in (
-        (cot_ref.at[:, pl.ds(0, ca)], S_RAW_A), (meta_out, S_META), (cotb, S_RAW_B), (sas, S_A), (sbs, S_B),
-        (relay_a, S_RELAY_A), (relay_b, S_RELAY_B), (sa.at[:, pl.ds(0, ne)], S_SIDE_A), (sb.at[pl.ds(0, ne)], S_SIDE_B),
-        (hr.at[pl.ds(0, 2 * nd + 1)], S_H), (hr.at[pl.ds(0, 2 * nd), main], S_MAIN),
-        (hr.at[pl.ds(0, 2 * nd), rest], S_REST), (lbuf.at[pl.ds(0, others)], S_LOAD),
+        (cot_ref.at[:, pl.ds(0, ca)], S_RAW_A), (meta_out, S_META), (cotb, S_RAW_B),
+        (sa.at[pl.ds(0, nm - 1), pl.ds(0, ne + 2)], S_A), (sb.at[pl.ds(0, ne + 2)], S_B),
+        (hr.at[pl.ds(0, 2 * nd + 1)], S_H), (hr.at[pl.ds(0, 2 * nd)], S_Q),
+        (load_out.at[0], S_LOAD), (load_out.at[1], S_LOAD + 1), (load_out.at[2], S_LOAD + 2),
     ):
         wait_in(ref, s_s.at[sem])
-    blocks_a = sa.at[0, pl.ds(0, ne)]
     for k in range(nm - 1):
-        for go, sems, ref in (
-            ((m - k >= 0) & has_up, (up_s, cu_s), cotb.at[0]), ((m + k < nm) & has_down, (dn_s, cd_s), cotb.at[0])
-        ):
-            wait_in(blocks_a, sems[0].at[k], go)
-            wait_in(ref, sems[1].at[k], go)
+        hops = pl.ds(0, k + 1)
+        for at, end, blocks, cols in ((m, nm - 1, up_s, cu_s), (nm - 1 - m, nm - 1, dn_s, cd_s)):
+            wait_in(sa.at[hops, pl.ds(0, ne)], blocks.at[0], at == k)
+            wait_in(cotb.at[hops], cols.at[0], at == k)
 
 
 def finish_kernel(
@@ -531,7 +529,8 @@
             pltpu.VMEM((most, ca), bf16),
             pltpu.VMEM((most, nm * cb), bf16),
             pltpu.VMEM((nm, toks, cb), bf16),
-            pltpu.VMEM((srcs, rows8, LANES), f32),
+            pltpu.VMEM((3, rows8, LANES), f32),
+            pltpu.VMEM((3, rows8, LANES), f32),
             pltpu.VMEM((nd, most, half), bf16),
             pltpu.VMEM((most, ca), bf16),
             pltpu.VMEM((most, nm * cb), bf16),
@@ -542,11 +541,11 @@
             pltpu.VMEM((3, half, 2 * whole), bf16),
             pltpu.VMEM((2, half, whole), bf16),
             dma((7,)),
-            dma((13,)),
-            dma((nm - 1,)),
-            dma((nm - 1,)),
-            dma((nm - 1,)),
-            dma((nm - 1,)),
+            dma((10,)),
+            dma((1,)),
+            dma((1,)),
+            dma((1,)),
+            dma((1,)),
             dma((nm, srcs)),
             dma((3,)),
             dma((nm,)),
@@ -554,7 +553,7 @@
             dma((6,)),
             dma((1,)),
             dma((nd,)),
-            dma((1,)),
+            dma((3,)),
         ],
         compiler_params=pltpu.CompilerParams(
             collective_id=0, has_side_effects=True, vmem_limit_bytes=VMEM_MOST - 12 * 1024 * 1024

time: 77.6 us -> 87 us (1.12)
  Pallas kernels: 76.6 us -> 86 us
    pallas_call x1, Pallas kernels: 72.7 us -> 82.2 us  [fast_body(): pl.pallas_call(functools.partial(exchange_kernel, dims), out_shape=(pltpu...]
where the time goes in v5:
time: 87 us; the launch traced here: 86.8 us
  Pallas kernels  86 us (99%)
    pallas_call x1, Pallas kernels, fast_body(): pl.pallas_call(functools.partial(exchange_kernel, dims), out_shape=(pltpu...  82.2 us
    pallas_call x1, Pallas kernels, fast_body(): pl.pallas_call(functools.partial(finish_kernel, nm), out_shape=(jax.Shape...  3.86 us

profile of v5, /device:TPU:0, one launch (start us, length us, event | category | flops | bytes accessed | tf_op | source)
XLA Modules:
  0.0 86.8 jit_solution(5836906893205267110)
XLA Ops:
  0.6 82.2 %shard_map.86 = (f32[4,896,384]{2,1,0:T(8,128)S(1)}, f32[896,512]{1,0:T(8,128)S(1)}, bf16[896,256]{1,0:T(8,128)(2,1)S(1)}, bf16[4,256,384]{2,1,0:T(8,128)(2,1)S(...) custom-call(bf16[384,2,1792]{2,1,0:T(2,128)(2,1)} %h_hbm.1, bf16[384,512]{1,0:T(8,128)(2,1)} %cot_hbm.1, ...), custom_call_target="tpu_custom_call" | custom-call | tf_op jit(solution)/shard_map/pallas_call | solution.py:505
  82.8 3.9 %shard_map.87 = (f32[1,896,2048]{2,1,0:T(8,128)}, f32[1,4]{1,0:T(1,128)}) custom-call(f32[4,896,384]{2,1,0:T(8,128)S(1)} %get-tuple-element.10.a_ref, f32[896,512]{1,0:T(8,128)S(1)} %get-tuple-element.11.b_ref, bf16[896,256]{1,0:T(8,128)(2,1)S(1)} %get-tuple-element.12.ht_ref, bf16[4,256,384]{2,1,0:T(8,128)(2,1)S(1)} %get-tuple-element.13.end_a, ...), custom_call_target="tpu_custom_call" | custom-call | tf_op jit(solution)/shard_map/pallas_call | solution.py:562

commit v6 on v5

--- a/solution.py
+++ b/solution.py
@@ -208,6 +208,12 @@
     pack_second = picker(tok_pos[2:3, :], tok_weight[2:3, :])
     sas[...] = pack_second(cot_ref[:, :ca])
     send(sas, sa.at[m, me], S_A, a_r.at[m, me], dev(ee=second))
+    in_order = (routes_ref[0:1, :] == row_id) | (routes_ref[1:2, :] == row_id)
+    counts = jnp.sum(jnp.where(in_order, live, 0.0), axis=1, keepdims=True)
+    lanes8 = lax.broadcasted_iota(jnp.int32, (rows8, LANES), 1) == row_id
+    load_out[0] = jnp.broadcast_to(jnp.sum(jnp.where(lanes8, counts, 0.0), axis=0, keepdims=True), (rows8, LANES))
+    send(load_out.at[0], load_in.at[0], S_LOAD, l_r.at[0], dev(ee=first))
+    send(load_out.at[0], load_in.at[1], S_LOAD, l_r.at[1], dev(ee=second))
 
     slot_flat = lax.broadcasted_iota(jnp.int32, (most, 2 * toks), 0)
     gap = lax.broadcasted_iota(jnp.int32, (toks, 2 * toks), 1) - 2 * lax.broadcasted_iota(
@@ -245,6 +251,8 @@
     pack_relay = picker(meta_in[3:4, :].astype(jnp.int32), meta_in[ne + 3 : ne + 4, :])
     relay_a[...] = pack_relay(raw_a[...])
     send(relay_a, sa.at[m, from_first], S_A, a_r.at[m, from_first], dev(ee=second))
+    wait_in(load_in.at[0], l_r.at[0])
+    send(load_in.at[0], load_in.at[2], S_LOAD, l_r.at[2], dev(ee=second))
     send(hs.at[2, d, main], hr.at[me, main], S_Q, h_r.at[H_SECOND], dev(dd=d, ee=second))
     pack_first = picker(meta_in[1:2, :].astype(jnp.int32), meta_in[ne + 1 : ne + 2, :])
     sa[m, from_first] = pack_first(raw_a[...])
@@ -254,22 +262,6 @@
     hr[me] = hs[0, d]
     pack_h(1)
 
-    in_order = (routes_ref[0:1, :] == row_id) | (routes_ref[1:2, :] == row_id)
-    counts = jnp.sum(jnp.where(in_order, live, 0.0), axis=1, keepdims=True)
-    lanes8 = lax.broadcasted_iota(jnp.int32, (rows8, LANES), 1) == row_id
-    load_out[0] = jnp.broadcast_to(jnp.sum(jnp.where(lanes8, counts, 0.0), axis=0, keepdims=True), (rows8, LANES))
-    partners = (dev(dd=side), dev(ee=first), dev(ee=second))
-
-    def add_load(n):
-        wait_in(load_in.at[n], l_r.at[n])
-        total = load_out[n] + load_in[n]
-        if n + 1 < len(partners):
-            load_out[n + 1] = total
-            send(load_out.at[n + 1], load_in.at[n + 1], S_LOAD + n + 1, l_r.at[n + 1], partners[n + 1])
-        else:
-            load_ref[...] = total
-
-    send(load_out.at[0], load_in.at[0], S_LOAD, l_r.at[0], partners[0])
     pass_cot(2)
     pass_cot(3)
     send(cotb, raw_b, S_RAW_B, rw_r.at[2], dev(ee=first))
@@ -352,7 +344,10 @@
     share_b(second)
     partner_a(1, e)
     unit(1, ht.at[0], own, True)
-    add_load(0)
+    for n in (1, 2):
+        wait_in(load_in.at[n], l_r.at[n])
+    load_out[1] = (load_out[0] + load_in[0]) + (load_in[1] + load_in[2])
+    send(load_out.at[1], load_in.at[3], S_LOAD, l_r.at[3], dev(dd=side))
     pass_on(2, e)
     wait_in(relay_h.at[1], rh_r.at[1])
     send(relay_h.at[1, main], hr.at[from_first, main], S_Q, h_r.at[H_DIAG], dev(dd=1, ee=second))
@@ -372,11 +367,11 @@
     pass_on(2, eg)
     partner_a(2, e)
     unit(2, ht.at[0], own, True)
-    add_load(1)
     pass_on(3, e)
     partner_a(3, e)
     unit(3, ht.at[0], own, True)
-    add_load(2)
+    wait_in(load_in.at[3], l_r.at[3])
+    load_ref[...] = load_out[1] + load_in[3]
     wait_h(slot(d, first), H_FIRST)
     wait_main(slot(d, second), H_SECOND)
     ht[2] = turn(slot(d, ex), slot(d, ey), 0, whole)
@@ -444,7 +439,7 @@
         (cot_ref.at[:, pl.ds(0, ca)], S_RAW_A), (meta_out, S_META), (cotb, S_RAW_B),
         (sa.at[pl.ds(0, nm - 1), pl.ds(0, ne + 2)], S_A), (sb.at[pl.ds(0, ne + 2)], S_B),
         (hr.at[pl.ds(0, 2 * nd + 1)], S_H), (hr.at[pl.ds(0, 2 * nd)], S_Q),
-        (load_out.at[0], S_LOAD), (load_out.at[1], S_LOAD + 1), (load_out.at[2], S_LOAD + 2),
+        (load_in, S_LOAD),
     ):
         wait_in(ref, s_s.at[sem])
     for k in range(nm - 1):
@@ -529,8 +524,8 @@
             pltpu.VMEM((most, ca), bf16),
             pltpu.VMEM((most, nm * cb), bf16),
             pltpu.VMEM((nm, toks, cb), bf16),
-            pltpu.VMEM((3, rows8, LANES), f32),
-            pltpu.VMEM((3, rows8, LANES), f32),
+            pltpu.VMEM((2, rows8, LANES), f32),
+            pltpu.VMEM((4, rows8, LANES), f32),
             pltpu.VMEM((nd, most, half), bf16),
             pltpu.VMEM((most, ca), bf16),
             pltpu.VMEM((most, nm * cb), bf16),
@@ -541,7 +536,7 @@
             pltpu.VMEM((3, half, 2 * whole), bf16),
             pltpu.VMEM((2, half, whole), bf16),
             dma((7,)),
-            dma((10,)),
+            dma((8,)),
             dma((1,)),
             dma((1,)),
             dma((1,)),
@@ -553,7 +548,7 @@
             dma((6,)),
             dma((1,)),
             dma((nd,)),
-            dma((3,)),
+            dma((4,)),
         ],
         compiler_params=pltpu.CompilerParams(
             collective_id=0, has_side_effects=True, vmem_limit_bytes=VMEM_MOST - 12 * 1024 * 1024

time: 87 us -> 76.3 us (0.88)
  Pallas kernels: 86 us -> 75.3 us
    pallas_call x1, Pallas kernels: 82.2 us -> 71.4 us  [fast_body(): pl.pallas_call(functools.partial(exchange_kernel, dims), out_shape=(pltpu...]
where the time goes in v6:
time: 76.3 us; the launch traced here: 76.1 us
  Pallas kernels  75.3 us (99%)
  between operations  0.8 us (1%)
    pallas_call x1, Pallas kernels, fast_body(): pl.pallas_call(functools.partial(exchange_kernel, dims), out_shape=(pltpu...  71.4 us
    pallas_call x1, Pallas kernels, fast_body(): pl.pallas_call(functools.partial(finish_kernel, nm), out_shape=(jax.Shape...  3.86 us

profile of v6, /device:TPU:0, one launch (start us, length us, event | category | flops | bytes accessed | tf_op | source)
XLA Modules:
  0.0 76.1 jit_solution(1715382369759717057)
XLA Ops:
  0.6 71.4 %shard_map.86 = (f32[4,896,384]{2,1,0:T(8,128)S(1)}, f32[896,512]{1,0:T(8,128)S(1)}, bf16[896,256]{1,0:T(8,128)(2,1)S(1)}, bf16[4,256,384]{2,1,0:T(8,128)(2,1)S(...) custom-call(bf16[384,2,1792]{2,1,0:T(2,128)(2,1)} %h_hbm.1, bf16[384,512]{1,0:T(8,128)(2,1)} %cot_hbm.1, ...), custom_call_target="tpu_custom_call" | custom-call | tf_op jit(solution)/shard_map/pallas_call | solution.py:500
  72.1 3.9 %shard_map.87 = (f32[1,896,2048]{2,1,0:T(8,128)}, f32[1,4]{1,0:T(1,128)}) custom-call(f32[4,896,384]{2,1,0:T(8,128)S(1)} %get-tuple-element.10.a_ref, f32[896,512]{1,0:T(8,128)S(1)} %get-tuple-element.11.b_ref, bf16[896,256]{1,0:T(8,128)(2,1)S(1)} %get-tuple-element.12.ht_ref, bf16[4,256,384]{2,1,0:T(8,128)(2,1)S(1)} %get-tuple-element.13.end_a, ...), custom_call_target="tpu_custom_call" | custom-call | tf_op jit(solution)/shard_map/pallas_call | solution.py:557

commit v7 on v6

--- a/solution.py
+++ b/solution.py
@@ -368,8 +368,6 @@
     partner_a(2, e)
     unit(2, ht.at[0], own, True)
     pass_on(3, e)
-    partner_a(3, e)
-    unit(3, ht.at[0], own, True)
     wait_in(load_in.at[3], l_r.at[3])
     load_ref[...] = load_out[1] + load_in[3]
     wait_h(slot(d, first), H_FIRST)
@@ -378,6 +376,8 @@
     for r in range(nm - 1):
         unit(r, ht.at[2], same)
     unit(B, ht.at[2], same)
+    partner_a(3, e)
+    unit(3, ht.at[0], own, True)
     pairs = hr.at[pl.ds(slot(0, eg), nd), main]
     wait_in(pairs, h_r.at[H_DIAG])
     ht[1] = turn(slot(0, eg), slot(1, eg), 0, whole)
@@ -385,8 +385,13 @@
         partner_a(r, eg)
         unit(r, ht.at[1], diag)
     share_b(eg)
-    partner_b(eg)
-    unit(B, ht.at[1], diag)
+    pass_on(3, first)
+
+    def diag_b():
+        partner_b(eg)
+        unit(B, ht.at[1], diag)
+
+    pl.when(d == 1)(diag_b)
     ends = (slot(side, second), second), (slot(side, first), first)
 
     def far(n, r):
@@ -401,7 +406,7 @@
     ht_far[0] = hr[ends[0][0], :whole].T
     for r in (0, 1, 2, B):
         far(0, r)
-    pass_on(3, first)
+    pl.when(d == 0)(diag_b)
     pass_on(3, second)
     unit(nm - 1, ht.at[2], same)
     far(0, nm - 1)

time: 76.3 us -> 76.3 us (level)
  no operation moved by 1% of the time
where the time goes in v7:
time: 76.3 us; the launch traced here: 76.1 us
  Pallas kernels  75.3 us (99%)
  between operations  0.8 us (1%)
    pallas_call x1, Pallas kernels, fast_body(): pl.pallas_call(functools.partial(exchange_kernel, dims), out_shape=(pltpu...  71.4 us
    pallas_call x1, Pallas kernels, fast_body(): pl.pallas_call(functools.partial(finish_kernel, nm), out_shape=(jax.Shape...  3.86 us

profile of v7, /device:TPU:0, one launch (start us, length us, event | category | flops | bytes accessed | tf_op | source)
XLA Modules:
  0.0 76.1 jit_solution(10349002604754603357)
XLA Ops:
  0.6 71.4 %shard_map.86 = (f32[4,896,384]{2,1,0:T(8,128)S(1)}, f32[896,512]{1,0:T(8,128)S(1)}, bf16[896,256]{1,0:T(8,128)(2,1)S(1)}, bf16[4,256,384]{2,1,0:T(8,128)(2,1)S(...) custom-call(bf16[384,2,1792]{2,1,0:T(2,128)(2,1)} %h_hbm.1, bf16[384,512]{1,0:T(8,128)(2,1)} %cot_hbm.1, ...), custom_call_target="tpu_custom_call" | custom-call | tf_op jit(solution)/shard_map/pallas_call | solution.py:505
  72.1 3.9 %shard_map.87 = (f32[1,896,2048]{2,1,0:T(8,128)}, f32[1,4]{1,0:T(1,128)}) custom-call(f32[4,896,384]{2,1,0:T(8,128)S(1)} %get-tuple-element.10.a_ref, f32[896,512]{1,0:T(8,128)S(1)} %get-tuple-element.11.b_ref, bf16[896,256]{1,0:T(8,128)(2,1)S(1)} %get-tuple-element.12.ht_ref, bf16[4,256,384]{2,1,0:T(8,128)(2,1)S(1)} %get-tuple-element.13.end_a, ...), custom_call_target="tpu_custom_call" | custom-call | tf_op jit(solution)/shard_map/pallas_call | solution.py:562
